TPU v7x, 32 devices: a whole 2x2x4 slice. The times are simulated.
32 devices in a mesh: groups: 2 (over y), tok: 8 (over z, core), head: 2 (over x), pair: 1.
Axes of the slice: x: 2, y: 2, z: 4, core: 2. Of those that a mesh axis runs over, the one named last changes fastest.
Arguments:
- queries: bfloat16 [2048, 4096], P(('groups', 'tok'), ('head', 'pair')), parts along dimension 0, may hold values from -6 to 6
- keys_values: bfloat16 [2048, 1024], P(('groups', 'tok'), ('head', 'pair')), parts along dimension 0, may hold values from -6 to 6
- sink_logits: float32 [64], P(('head', 'pair')), may hold values from -2 to 3
- residual: bfloat16 [2048, 2880], P(('groups', 'tok')), parts along dimension 0, may hold values from -60 to 60
- out_weight: bfloat16 [4096, 2880], P(('head', 'pair')), may hold values from -0.09375 to 0.09375
- norm_gain: float32 [2880], replicated, may hold values from 0.5 to 1.5
- expert_ids: int32 [2048, 4], P(('groups', 'tok')), parts along dimension 0, may hold values from 0 to 7, all different within a row; in each aligned block of 128 rows (0 to 127, 128 to 255, ...) at most 80 rows name the same one
- route_weights: float32 [2048, 4], P(('groups', 'tok')), parts along dimension 0, may hold values from 0.1 to 1
- gate_up: bfloat16 [8, 2880, 2, 1440], P('tok', None, None, ('head', 'pair')), may hold values from -0.109375 to 0.109375
- down_weight: bfloat16 [8, 1440, 2880], P('tok', ('head', 'pair')), may hold values from -0.21875 to 0.21875
Outputs:
- layer_output: bfloat16 [2048, 2880], P(('groups', 'tok'), ('head', 'pair')), parts along dimension 0
There are 2 independent parts, one for each index of `groups`. A program takes and returns all parts, laid end to end along the dimension named above; an argument that names none is the same for every part. Nothing has to cross between parts.
Inputs may be any that keep to these rules, and one draw needn't show every extreme that they name: `expert_ids`: in each aligned block of 128 rows (the rows of one index of tok), a row names 4 different experts and no expert is named by more than 80 rows.
All inputs are finite; a program needn't handle non-finite values.
Results may differ from a plain program's by a relative error of at most 0.01.
Values may be sent and summed in bfloat16 or wider, within the bound.
A program may use at most 128 MiB of HBM per device.

v0:
```python
import functools

import jax
import jax.numpy as jnp
from jax import lax
from jax.experimental import pallas as pl
from jax.experimental.pallas import tpu as pltpu
from jax.sharding import PartitionSpec as P

HEAD_DIM = 64

MESH_ID = pl.DeviceIdType.MESH


def moe_kernel(
    dims,
    parts_ref,
    residual_ref,
    gain_ref,
    tail_ref,
    gate_hbm,
    down_hbm,
    out_ref,
    gate_w,
    down_w,
    rows,
    part,
    from_core,
    kept,
    from_peer,
    hop,
    from_right,
    from_left,
    peer_parts,
    stream,
    squares,
    peer_squares,
    acc,
    parts_send,
    parts_recv,
    squares_send,
    squares_recv,
    load_sem,
    row_recv,
    row_right,
    row_left,
    row_peer,
    row_core,
    part_send,
    part_recv,
    peer_send,
    peer_recv,
    hop_send,
    right_recv,
    left_recv,
):
    chips, cores, shares, pairs, width = dims
    tok = lax.axis_index("tok")
    z = tok // cores
    c = tok % cores
    mine = lax.axis_index("head") * pairs + lax.axis_index("pair")
    other = cores - 1 - c

    def tok_id(chip, core):
        return {"tok": chip * cores + core}

    def peer_id(share):
        return {"head": share // pairs, "pair": share % pairs}

    def remote(src, dst, send, recv, target):
        return pltpu.make_async_remote_copy(
            src_ref=src, dst_ref=dst, send_sem=send, recv_sem=recv,
            device_id=target, device_id_type=MESH_ID,
        )

    loads = [
        pltpu.make_async_copy(gate_hbm, gate_w.at[:, :, pl.ds(0, width)], load_sem.at[0]),
        pltpu.make_async_copy(down_hbm, down_w, load_sem.at[1]),
    ]
    for load in loads:
        load.start()

    barrier = pltpu.get_barrier_semaphore()

    @pl.when(z > 0)
    def _():
        pl.semaphore_signal(barrier, 1, device_id=tok_id(z - 1, c), device_id_type=MESH_ID)

    @pl.when(z < chips - 1)
    def _():
        pl.semaphore_signal(barrier, 1, device_id=tok_id(z + 1, c), device_id_type=MESH_ID)

    if cores > 1:
        pl.semaphore_signal(barrier, 1, device_id=tok_id(z, other), device_id_type=MESH_ID)
    for d in range(1, shares):
        pl.semaphore_signal(
            barrier, 1, device_id=peer_id((mine + d) % shares), device_id_type=MESH_ID
        )
    sides = jnp.where(z > 0, 1, 0) + jnp.where(z < chips - 1, 1, 0)
    pl.semaphore_wait(barrier, sides + (cores - 1) + (shares - 1))

    def parts_copy(d):
        share = (mine + d) % shares
        return remote(
            parts_ref.at[share], peer_parts.at[mine], parts_send.at[d - 1],
            parts_recv.at[mine], peer_id(share),
        )

    def squares_copy(d):
        return remote(
            squares, peer_squares.at[mine], squares_send.at[d - 1],
            squares_recv.at[mine], peer_id((mine + d) % shares),
        )

    for d in range(1, shares):
        parts_copy(d).start()
    gate_w[:, :, width:, :] = jnp.zeros(
        gate_w.shape[:2] + (gate_w.shape[2] - width, gate_w.shape[3]), jnp.bfloat16
    )
    stream[...] = residual_ref[...].astype(jnp.float32) + parts_ref[mine].astype(jnp.float32)
    for d in range(1, shares):
        share = (mine + d) % shares
        slot = peer_parts.at[share]
        pltpu.make_async_copy(slot, slot, parts_recv.at[share]).wait()
        stream[...] += peer_parts[share].astype(jnp.float32)
    own = stream[...]
    square = jnp.sum(own * own, axis=1, keepdims=True)
    squares[...] = jnp.broadcast_to(square, squares.shape)
    for d in range(1, shares):
        squares_copy(d).start()
    total_square = squares[...]
    for d in range(1, shares):
        share = (mine + d) % shares
        slot = peer_squares.at[share]
        pltpu.make_async_copy(slot, slot, squares_recv.at[share]).wait()
        total_square += peer_squares[share]
    inverse = lax.rsqrt(total_square[:, :1] / (shares * width) + 1e-05)
    normed = stream[...] * inverse * gain_ref[...] + tail_ref[...].astype(jnp.float32)
    rows[z, mine, c] = normed.astype(jnp.bfloat16)

    near = jnp.minimum(z, chips - 1 - z)

    def chip_at(i):
        inner = jnp.where(i % 2 == 1, z - (i + 1) // 2, z + i // 2)
        outer = jnp.where(z < chips - 1 - z, i, chips - 1 - i)
        return jnp.where(i <= 2 * near, inner, outer)

    def row_copy(chip, share, core, send, target):
        slot = rows.at[chip, share, core]
        return remote(slot, slot, send, row_recv.at[chip, core, share], target)

    def go_right(chip):
        return (chip <= z) & (z < chips - 1)

    def go_left(chip):
        return (chip >= z) & (z > 0)

    def right_copy(chip):
        return row_copy(chip, mine, c, row_right.at[chip], tok_id(z + 1, c))

    def left_copy(chip):
        return row_copy(chip, mine, c, row_left.at[chip], tok_id(z - 1, c))

    def peer_copy(chip, d):
        return row_copy(chip, mine, c, row_peer.at[chip, d - 1], peer_id((mine + d) % shares))

    def core_copy(chip, share):
        return row_copy(chip, share, c, row_core.at[chip, share], tok_id(z, other))

    def row_wait(chip, share, core):
        slot = rows.at[chip, share, core]
        pltpu.make_async_copy(slot, slot, row_recv.at[chip, core, share]).wait()

    def forward(i):
        chip = chip_at(i)

        @pl.when(go_right(chip))
        def _():
            right_copy(chip).start()

        @pl.when(go_left(chip))
        def _():
            left_copy(chip).start()

        for d in range(1, shares):
            peer_copy(chip, d).start()
        if cores > 1:
            core_copy(chip, mine).start()

    forward(0)
    loads[0].wait()
    loads[1].wait()

    tail = (width // 128) * 128
    wide = rows.shape[-1]
    depth = rows.shape[-2]
    experts = chips * cores
    tail_lane = tail + lax.broadcasted_iota(jnp.int32, (cores * depth, wide - tail), 1)
    weight_lane = (tail_lane == width + tok) | (tail_lane == width + experts + tok)

    def kept_at(chip, share):
        return kept.at[chip, share] if cores > 1 else part.at[chip, share, 0]

    def part_copy(chip, share):
        return remote(
            part.at[chip, share, other], from_core.at[chip, share],
            part_send.at[chip, share], part_recv.at[chip, share], tok_id(z, other),
        )

    def sum_copy(chip, d):
        share = (mine + d) % shares
        return remote(
            kept_at(chip, share), from_peer.at[chip, mine],
            peer_send.at[chip, d - 1], peer_recv.at[chip, mine], peer_id(share),
        )

    def compute(i, carry):
        @pl.when(i + 1 < chips)
        def _():
            row_wait(chip_at(i + 1), mine, c)
            forward(i + 1)

        chip = chip_at(i)
        for d in range(1, shares):
            share = (mine + d) % shares
            row_wait(chip, share, c)
            if cores > 1:
                core_copy(chip, share).start()
        if cores > 1:
            for share in range(shares):
                row_wait(chip, share, other)
        gate = jnp.zeros((cores * depth, gate_w.shape[-1]), jnp.float32)
        up = gate
        for share in range(shares):
            block = rows[chip, share].reshape(cores * depth, wide)
            gate += jnp.dot(block, gate_w[0, share], preferred_element_type=jnp.float32)
            up += jnp.dot(block, gate_w[1, share], preferred_element_type=jnp.float32)
        active = (gate * jax.nn.sigmoid(1.702 * gate) * (up + 1.0)).astype(jnp.bfloat16)
        ends = rows[chip, 0, :, :, tail:].reshape(cores * depth, wide - tail).astype(jnp.float32)
        weight = jnp.sum(jnp.where(weight_lane, ends, 0.0), axis=1, keepdims=True)
        for share in range(shares):
            out = jnp.dot(active, down_w[share], preferred_element_type=jnp.float32)
            out = (out * weight).astype(jnp.bfloat16)
            part[chip, share] = out.reshape(cores, depth, width)
            if cores > 1:
                part_copy(chip, share).start()
        for share in range(shares):
            if cores > 1:
                part_copy(chip, share).wait_recv()
                total = part[chip, share, c].astype(jnp.float32)
                total += from_core[chip, share].astype(jnp.float32)
                kept[chip, share] = total.astype(jnp.bfloat16)
        for d in range(1, shares):
            sum_copy(chip, d).start()
        return carry

    lax.fori_loop(0, chips, compute, 0)

    def right_hop(chip):
        return remote(
            hop.at[chip], from_left.at[chip], hop_send.at[chip], left_recv.at[chip],
            tok_id(z + 1, c),
        )

    def left_hop(chip):
        return remote(
            hop.at[chip], from_right.at[chip], hop_send.at[chip], right_recv.at[chip],
            tok_id(z - 1, c),
        )

    def hop_wait(buffer, sem, chip):
        pltpu.make_async_copy(buffer.at[chip], buffer.at[chip], sem.at[chip]).wait()

    def give_back(j, carry):
        chip = chip_at(chips - 1 - j)
        total = kept_at(chip, mine)[...].astype(jnp.float32)
        for d in range(1, shares):
            share = (mine + d) % shares
            slot = from_peer.at[chip, share]
            pltpu.make_async_copy(slot, slot, peer_recv.at[chip, share]).wait()
            total += from_peer[chip, share].astype(jnp.float32)
        acc[...] = total

        @pl.when((chip <= z) & (z < chips - 1))
        def _():
            hop_wait(from_right, right_recv, chip)
            acc[...] += from_right[chip].astype(jnp.float32)

        @pl.when((chip >= z) & (z > 0))
        def _():
            hop_wait(from_left, left_recv, chip)
            acc[...] += from_left[chip].astype(jnp.float32)

        @pl.when(chip == z)
        def _():
            out_ref[...] = (stream[:, :width] + acc[...]).astype(jnp.bfloat16)

        @pl.when(chip != z)
        def _():
            hop[chip] = acc[...].astype(jnp.bfloat16)

        @pl.when(chip < z)
        def _():
            left_hop(chip).start()

        @pl.when(chip > z)
        def _():
            right_hop(chip).start()

        return carry

    lax.fori_loop(0, chips, give_back, 0)

    def drain(chip, carry):
        @pl.when(go_right(chip))
        def _():
            right_copy(chip).wait_send()

        @pl.when(go_left(chip))
        def _():
            left_copy(chip).wait_send()

        for d in range(1, shares):
            peer_copy(chip, d).wait_send()
            sum_copy(chip, d).wait_send()
        if cores > 1:
            for share in range(shares):
                core_copy(chip, share).wait_send()
                part_copy(chip, share).wait_send()

        @pl.when(chip < z)
        def _():
            left_hop(chip).wait_send()

        @pl.when(chip > z)
        def _():
            right_hop(chip).wait_send()

        return carry

    lax.fori_loop(0, chips, drain, 0)
    for d in range(1, shares):
        parts_copy(d).wait_send()
        squares_copy(d).wait_send()


def moe(dims, parts, residual, gain, tail, gate_w, down_w):
    chips, cores, shares, pairs, width = dims
    depth, wide = residual.shape
    hidden = down_w.shape[1]
    bf16 = jnp.bfloat16
    dma = pltpu.SemaphoreType.DMA
    return pl.pallas_call(
        functools.partial(moe_kernel, dims),
        out_shape=jax.ShapeDtypeStruct((depth, width), jnp.bfloat16),
        in_specs=[pl.BlockSpec(memory_space=pltpu.VMEM)] * 4
        + [
            pl.BlockSpec(memory_space=pl.ANY),
            pl.BlockSpec(memory_space=pl.ANY),
        ],
        out_specs=pl.BlockSpec(memory_space=pltpu.VMEM),
        scratch_shapes=[
            pltpu.VMEM((2, shares, wide, hidden), bf16),
            pltpu.VMEM(down_w.shape, bf16),
            pltpu.VMEM((chips, shares, cores, depth, wide), bf16),
            pltpu.VMEM((chips, shares, cores, depth, width), bf16),
            pltpu.VMEM((chips, shares, depth, width) if cores > 1 else (8, 128), bf16),
            pltpu.VMEM((chips, shares, depth, width) if cores > 1 else (8, 128), bf16),
            pltpu.VMEM((chips, shares, depth, width), bf16),
            pltpu.VMEM((chips, depth, width), bf16),
            pltpu.VMEM((chips, depth, width), bf16),
            pltpu.VMEM((chips, depth, width), bf16),
            pltpu.VMEM((shares, depth, wide), bf16),
            pltpu.VMEM((depth, wide), jnp.float32),
            pltpu.VMEM((depth, 128), jnp.float32),
            pltpu.VMEM((shares, depth, 128), jnp.float32),
            pltpu.VMEM((depth, width), jnp.float32),
            dma((max(shares - 1, 1),)),
            dma((shares,)),
            dma((max(shares - 1, 1),)),
            dma((shares,)),
            dma((2,)),
            dma((chips, cores, shares)),
            dma((chips,)),
            dma((chips,)),
            dma((chips, max(shares - 1, 1))),
            dma((chips, shares)),
            dma((chips, shares)),
            dma((chips, shares)),
            dma((chips, max(shares - 1, 1))),
            dma((chips, shares)),
            dma((chips,)),
            dma((chips,)),
            dma((chips,)),
        ],
        compiler_params=pltpu.CompilerParams(
            collective_id=0, has_side_effects=True, vmem_limit_bytes=60 * 1024 * 1024
        ),
        cost_estimate=pl.CostEstimate(
            flops=6 * chips * cores * depth * shares * width * hidden,
            bytes_accessed=6 * shares * width * hidden,
            transcendentals=0,
        ),
    )(parts, residual, gain, tail, gate_w, down_w)


def per_device(
    queries,
    keys_values,
    sink_logits,
    residual,
    out_weight,
    norm_gain,
    expert_ids,
    route_weights,
    gate_up,
    down_weight,
):
    tok_rows = queries.shape[0]
    kv_groups = keys_values.shape[1] // (2 * HEAD_DIM)
    local_heads = queries.shape[1] // HEAD_DIM
    repeat = local_heads // kv_groups
    position = lax.axis_index("tok") * tok_rows + jnp.arange(tok_rows, dtype=jnp.int32)
    grouped = queries.reshape(tok_rows, kv_groups, repeat, HEAD_DIM)
    start_max = jnp.broadcast_to(
        sink_logits.reshape(kv_groups, repeat)[:, :, None], (kv_groups, repeat, tok_rows)
    )
    start_totals = jnp.ones((kv_groups, repeat, tok_rows), jnp.float32)
    start_accum = jnp.zeros((kv_groups, repeat, tok_rows, HEAD_DIM), jnp.float32)
    key_piece = lax.all_gather(keys_values, "tok", axis=0, tiled=True)
    hidden = down_weight.shape[1]
    shares = lax.axis_size(("head", "pair"))
    share = out_weight.shape[1] // shares
    gate_w = jnp.transpose(gate_up[0], (1, 0, 2)).reshape(2, shares, share, hidden)
    down_w = jnp.transpose(down_weight[0].reshape(hidden, shares, share), (1, 0, 2))
    key_piece, gate_w, down_w = lax.optimization_barrier((key_piece, gate_w, down_w))
    totals = start_totals
    accum = start_accum
    count = key_piece.shape[0]
    split_piece = key_piece.reshape(count, kv_groups, 2, HEAD_DIM)
    scores = (
        jnp.einsum(
            "tgrd,ngd->grtn", grouped, split_piece[:, :, 0], preferred_element_type=jnp.float32
        )
        * 0.125
    )
    key_position = jnp.arange(count, dtype=jnp.int32)
    allowed = key_position[None, :] <= position[:, None]
    scores = jnp.where(allowed, scores, jnp.float32(-1e30))
    new_max = jnp.maximum(start_max, jnp.max(scores, axis=-1))
    decay = jnp.exp(start_max - new_max)
    weights = jnp.exp(scores - new_max[..., None])
    totals = totals * decay + jnp.sum(weights, axis=-1)
    update = jnp.einsum(
        "grtn,ngd->grtd",
        weights.astype(jnp.bfloat16),
        split_piece[:, :, 1],
        preferred_element_type=jnp.float32,
    )
    accum = accum * decay[..., None] + update
    final_max, totals, accum = (new_max, totals, accum)
    attended = (accum / totals[..., None]).astype(jnp.bfloat16)
    attended = jnp.transpose(attended, (2, 0, 1, 3)).reshape(tok_rows, local_heads * HEAD_DIM)
    width = out_weight.shape[1]
    share = width // lax.axis_size(("head", "pair"))
    column_start = lax.axis_index(("head", "pair")) * share
    partial_value = jnp.dot(attended, out_weight, preferred_element_type=jnp.float32)
    experts = lax.axis_size("tok")
    pairs = lax.axis_size("pair")
    cores = 2 // pairs
    shares = width // share
    wide = -(-(share + 2 * experts) // 128) * 128
    expert = jnp.arange(experts, dtype=jnp.int32)
    routed = expert_ids[:, :, None] == expert
    dense = jnp.sum(jnp.where(routed, route_weights[:, :, None], 0.0), axis=1)
    high = lax.reduce_precision(dense, 8, 7)
    weights = jnp.concatenate([high, dense - high], axis=1).astype(jnp.bfloat16)
    tail = jnp.pad(weights, ((0, 0), (share, wide - share - 2 * experts)))
    spare = (0, wide - share)
    parts = jnp.transpose(
        partial_value.astype(jnp.bfloat16).reshape(tok_rows, shares, share), (1, 0, 2)
    )
    parts = jnp.pad(parts, ((0, 0), (0, 0), spare))
    own_residual = jnp.pad(
        lax.dynamic_slice_in_dim(residual, column_start, share, 1), ((0, 0), spare)
    )
    own_gain = jnp.pad(lax.dynamic_slice_in_dim(norm_gain, column_start, share, 0), spare)
    return moe(
        (experts // cores, cores, shares, pairs, share),
        parts, own_residual, own_gain[None, :], tail, gate_w, down_w,
    )


def solution(mesh):
    placed = (
        P(("groups", "tok"), ("head", "pair")),
        P(("groups", "tok"), ("head", "pair")),
        P(("head", "pair")),
        P(("groups", "tok"), None),
        P(("head", "pair"), None),
        P(),
        P(("groups", "tok"), None),
        P(("groups", "tok"), None),
        P("tok", None, None, ("head", "pair")),
        P("tok", ("head", "pair"), None),
    )
    return jax.shard_map(
        per_device,
        mesh=mesh,
        in_specs=placed,
        out_specs=P(("groups", "tok"), ("head", "pair")),
        check_vma=False,
    )
```

profile of v0, /device:TPU:0, one launch (start us, length us, event | category | flops | bytes accessed | tf_op | source)
XLA Modules:
  0.0 193.2 jit_solution(7058467046188529321)
XLA Ops:
  6.5 0.0 copy-start
  6.5 0.0 all-gather.2.cloned.1.call-start
  6.5 1.7 copy.45
  8.3 0.0 all-gather.2.cloned.1.call-update
  8.3 0.0 copy-start.2
  8.3 0.0 copy-start.7
  8.3 0.0 copy-start.4
  8.3 0.0 copy-start.5
  8.4 0.0 copy-start.6
  8.4 12.0 %copy.46 = bf16[2,2880,720]{2,1,0:T(8,128)(2,1)} copy(bf16[2,2880,720]{1,2,0:T(8,128)(2,1)} %bitcast.59) | data formatting | bytes 16588800 | tf_op jit(solution)/shard_map/transpose | solution.py:434
  20.3 6.5 %copy.47 = bf16[1,720,2880]{1,2,0:T(8,128)(2,1)} copy(bf16[1,720,2880]{2,1,0:T(8,128)(2,1)} %param.19) | data formatting | bytes 8294400 | tf_op args[9]
  26.9 6.5 %copy.48 = bf16[720,2,1440]{2,0,1:T(8,128)(2,1)} copy(bf16[720,2,1440]{0,2,1:T(8,128)(2,1)} %bitcast.57) | data formatting | bytes 8294400 | tf_op jit(solution)/shard_map/reshape;squeeze | solution.py:435
  33.4 0.0 copy-done.2
  33.4 0.3 copy.50
  33.7 0.0 copy-done.7
  33.7 0.1 broadcast_in_dim.41
  33.8 0.0 copy-done
  33.8 0.2 copy.62
  34.0 0.0 copy-done.4
  34.0 0.1 dynamic_slice.7
  34.1 0.6 broadcast_in_dim.46.gain_ref
  34.7 0.0 copy-done.5
  34.7 0.0 copy-done.6
  34.7 0.1 copy.55
  34.9 0.8 pad.17.residual_ref
  35.6 0.8 pad.19.tail_ref
  36.5 0.1 iota_compare_fusion
  36.6 0.0 all-gather.2.cloned.1.call-done
  36.6 0.0 copy-start.3
  36.6 8.2 %fusion.2 = (f32[4,8,128]{2,1,0:T(8,128)S(1)}, f32[4,1024,128,8]{2,1,3,0:T(8,128)}) fusion(pred[128,1024]{0,1:T(8,128)(4,1)S(1)} %iota_compare_fusion, bf16[128,4,8,64]{0,3,2,1:T(8,128)(2,1)S(1)} %bitcast.62, bf16[1024,4,2,64]{0,3,2,1:T(8,128)(2,1)} %bitcast.64), kind=kOutput, calls=%fused_computation.4 | convolution fusion | flops 549449728 | bytes 17973248 | tf_op jit(solution)/shard_map/tgrd,ngd->grtn/dot_general | solution.py:442
  44.8 0.1 broadcast_maximum_fusion
  44.9 9.2 %fusion = f32[4,8,128]{2,1,0:T(8,128)S(1)} fusion(f32[4,1024,128,8]{2,1,3,0:T(8,128)} %get-tuple-element.16, f32[4,8,128]{2,1,0:T(8,128)S(1)} %broadcast_maximum_fusion, pred[128,1024]{0,1:T(8,128)(4,1)S(1)} %iota_compare_fusion), kind=kLoop, calls=%fused_computation.2 | loop fusion | flops 16773120 | bytes 16941056 | tf_op jit(solution)/shard_map/reduce_sum | solution.py:453
  54.0 0.0 slice-start
  54.0 0.1 multiply_bitcast_fusion
  54.1 0.0 copy-done.3
  54.1 0.0 slice-start.1
  54.1 0.0 slice-start.2
  54.2 8.1 %divide_convert_fusion = bf16[128,4,8,64]{0,3,2,1:T(8,128)(2,1)S(1)} fusion(f32[4,1024,128,8]{2,1,3,0:T(8,128)} %get-tuple-element.16, f32[4,8,128]{2,1,0:T(8,128)S(1)} %broadcast_maximum_fusion, pred[128,1024]{0,1:T(8,128)(4,1)S(1)} %iota_compare_fusion, bf16[1024,4,2,64]{0,3,2,1:T(8,128)(2,1)S(1)} %bitcast.65, f32[128,4,8]{0,2,1:T(8,128)S(1)} %get-tuple-element.12, ...), kind=kOutput, calls=%fused_computation.10 | convolution fusion | flops 554434560 | bytes 18006016 | tf_op jit(solution)/shard_map/grtn,ngd->grtd/dot_general | solution.py:454
  62.3 0.0 slice-done
  62.3 0.0 slice-done.1
  62.3 1.0 slice-done.2
  63.3 3.2 %convolution_convert_fusion = bf16[128,2880]{0,1:T(8,128)(2,1)S(1)} fusion(bf16[2048,2880]{0,1:T(8,128)(2,1)S(1)} %bitcast.67, bf16[128,2048]{0,1:T(8,128)(2,1)S(1)} %bitcast.68), kind=kOutput, calls=%fused_computation.7 | convolution fusion | flops 1510318080 | bytes 13058048 | tf_op jit(solution)/shard_map/dot_general | solution.py:467
  66.5 0.3 copy.53
  66.8 0.0 copy-start.1
  66.8 1.0 pad.16.parts_ref
  67.8 116.7 %shard_map.100 = bf16[128,1440]{1,0:T(8,128)(2,1)} custom-call(bf16[2,128,1536]{2,1,0:T(8,128)(2,1)} %pad.16.parts_ref, bf16[128,1536]{1,0:T(8,128)(2,1)} %pad.17.residual_ref, f32[1,1536]{1,0:T(1,128)} %broadcast_in_dim.46.gain_ref, bf16[128,1536]{1,0:T(8,128)(2,1)} %pad.19.tail_ref, bf16[2,2,1440,720]{3,2,1,0:T(8,128)(2,1)} %bitcast.58, ...), custom_call_target="tpu_custom_call" | custom-call | flops 12740198400 | bytes 12441600 | tf_op jit(solution)/shard_map/pallas_call | solution.py:353
  184.4 1.9 copy.56
  186.4 0.0 copy-done.1
  (7 shorter events, 0.1 us)
Async XLA Ops:
  6.5 27.2 %copy-start = (bf16[128,2880]{0,1:T(8,128)(2,1)S(1)}, bf16[128,2880]{0,1:T(8,128)(2,1)}, u32[]{:S(2)}) copy-start(bf16[128,2880]{0,1:T(8,128)(2,1)} %param.13) | copy-start | bytes 2211844
  6.5 30.1 %all-gather.2.cloned.1.call-start = ((), (), s32[]{:S(2)}) async-start(), calls=%async_computation | async-start | bytes 1179648 | tf_op jit(solution)/shard_map/all_gather | solution.py:430
  8.3 25.1 %copy-start.2 = (bf16[128,2048]{1,0:T(8,128)(2,1)S(1)}, bf16[128,2048]{1,0:T(8,128)(2,1)}, u32[]{:S(2)}) copy-start(bf16[128,2048]{1,0:T(8,128)(2,1)} %param.10) | copy-start | bytes 1572868
  8.3 25.4 %copy-start.7 = (f32[32]{0:T(128)S(1)}, f32[32]{0:T(128)}, u32[]{:S(2)}) copy-start(f32[32]{0:T(128)} %param.12) | copy-start | bytes 388
  8.3 25.7 %copy-start.4 = (f32[2880]{0:T(1024)S(1)}, f32[2880]{0:T(1024)}, u32[]{:S(2)}) copy-start(f32[2880]{0:T(1024)} %param.15) | copy-start | bytes 34564
  8.3 26.4 %copy-start.5 = (f32[128,4]{0,1:T(4,128)S(1)}, f32[128,4]{0,1:T(4,128)}, u32[]{:S(2)}) copy-start(f32[128,4]{0,1:T(4,128)} %param.17) | copy-start | bytes 6148
  8.4 26.4 %copy-start.6 = (s32[128,4]{0,1:T(4,128)S(1)}, s32[128,4]{0,1:T(4,128)}, u32[]{:S(2)}) copy-start(s32[128,4]{0,1:T(4,128)} %param.16) | copy-start | bytes 6148
  36.6 17.5 %copy-start.3 = (bf16[1024,512]{0,1:T(8,128)(2,1)S(1)}, bf16[1024,512]{0,1:T(8,128)(2,1)}, u32[]{:S(2)}) copy-start(bf16[1024,512]{0,1:T(8,128)(2,1)} %all-gather.2.cloned.1.call-done) | copy-start | bytes 3145732
  54.0 8.3 %slice-start = ((s8[11796480]{0:T(1024)(128)(4,1)}), s8[4194304]{0:T(1024)(128)(4,1)S(1)}, s32[]{:S(2)}) async-start(s8[11796480]{0:T(1024)(128)(4,1)} %bitcast.66), calls=%async_computation.1 | async-start | bytes 8388608
  54.1 8.2 %slice-start.1 = ((s8[11796480]{0:T(1024)(128)(4,1)}), s8[4194304]{0:T(1024)(128)(4,1)S(1)}, s32[]{:S(2)}) async-start(s8[11796480]{0:T(1024)(128)(4,1)} %bitcast.66), calls=%async_computation.2 | async-start | bytes 8388608
  54.1 9.1 %slice-start.2 = ((s8[11796480]{0:T(1024)(128)(4,1)}), s8[3407872]{0:T(1024)(128)(4,1)S(1)}, s32[]{:S(2)}) async-start(s8[11796480]{0:T(1024)(128)(4,1)} %bitcast.66), calls=%async_computation.3 | async-start | bytes 6815744
  66.8 119.6 %copy-start.1 = (bf16[128,2880]{0,1:T(8,128)(2,1)S(1)}, bf16[128,2880]{0,1:T(8,128)(2,1)}, u32[]{:S(2)}) copy-start(bf16[128,2880]{0,1:T(8,128)(2,1)} %param.13) | copy-start | bytes 2211844
Sparse Core Ops, SparseCore 0:
  8.9 26.5 all-gather.1
where the time goes:
time: 194 us; the launch traced here: 193 us
  Pallas kernels  117 us (60%)
  local copies, waits for them, and re-layouts  33.9 us (17%)
  matrix products  19.5 us (10%)
  between operations  13.6 us (7%)
  other arithmetic  9.44 us (5%)
    pallas_call x1, Pallas kernels, moe(): pl.pallas_call(functools.partial(moe_kernel, dims), out_shape=jax.ShapeDt...  117 us
    transpose x1, local copies, waits for them, and re-layouts, per_device(): jnp.transpose(gate_up[0], (1, 0, 2)).reshape(2, shares, share, hidden)  12 us
    unnamed x26, local copies, waits for them, and re-layouts  9.74 us
    reduce_sum x1, other arithmetic, per_device(): totals = totals * decay + jnp.sum(weights, axis=-1)  9.17 us
    dot_general x1, matrix products, per_device(): jnp.einsum('tgrd,ngd->grtn', grouped, split_piece[:, :, 0], preferred_ele...  8.16 us
    dot_general x1, matrix products, per_device(): jnp.einsum('grtn,ngd->grtd', weights.astype(jnp.bfloat16), split_piece[:,...  8.13 us
    another operation x1, local copies, waits for them, and re-layouts, per_device(): down_weight[0].reshape(hidden, shares, share)  6.54 us
  transfers between devices with their start and end apart: 1, of which 0 were waited for; matrix products, arithmetic and copies ran while one was open for 15% of the time, Pallas kernels for 0%

commit v1 on v0

--- a/solution.py
+++ b/solution.py
@@ -10,6 +10,8 @@
 HEAD_DIM = 64
 
 MESH_ID = pl.DeviceIdType.MESH
+
+VMEM_BYTES = 67_043_328
 
 
 def moe_kernel(
@@ -491,6 +493,721 @@
     )
 
 
+def layer_kernel(
+    dims,
+    sink_ref,
+    ids_ref,
+    route_ref,
+    gain_ref,
+    query_hbm,
+    kv_hbm,
+    residual_hbm,
+    project_hbm,
+    gate_hbm,
+    down_hbm,
+    out_ref,
+    query_v,
+    query_t,
+    kvs,
+    row_max,
+    row_total,
+    accum,
+    attended,
+    residual_v,
+    project_w,
+    gate_w,
+    down_v,
+    down_t,
+    gain_cols,
+    stream,
+    parts,
+    peer_parts,
+    rows,
+    meta,
+    hidden,
+    active,
+    part,
+    kept,
+    from_core,
+    cross,
+    from_peer,
+    hop,
+    from_left,
+    from_right,
+    load_sem,
+    kv_recv,
+    kv_core_send,
+    kv_up_send,
+    parts_send,
+    parts_recv,
+    row_recv,
+    row_up,
+    row_down,
+    row_core,
+    row_peer,
+    meta_recv,
+    meta_up,
+    meta_down,
+    meta_core,
+    part_send,
+    part_recv,
+    peer_send,
+    peer_recv,
+    hop_send,
+    left_recv,
+    right_recv,
+):
+    chips, pairs, chunk, piece = dims
+    cores = 2
+    width, depth = residual_hbm.shape
+    kv_groups = kvs.shape[1]
+    repeat = query_t.shape[2] // depth
+    half = width // 2
+    f32, bf16 = jnp.float32, jnp.bfloat16
+    full = width // chunk
+    tail = width - full * chunk
+    own = full // 2
+    shared = full - 2 * own
+    pieces = half // piece
+    last = chips - 1
+
+    tok = lax.axis_index("tok")
+    z = tok // cores
+    c = tok % cores
+    x = lax.axis_index("head") * pairs + lax.axis_index("pair")
+    peer = {"head": (1 - x) // pairs, "pair": (1 - x) % pairs}
+    other = {"tok": z * cores + (1 - c)}
+    above = {"tok": (z + 1) * cores + c}
+    below = {"tok": (z - 1) * cores + c}
+
+    def remote(src, dst, send, recv, target):
+        return pltpu.make_async_remote_copy(
+            src_ref=src, dst_ref=dst, send_sem=send, recv_sem=recv,
+            device_id=target, device_id_type=MESH_ID,
+        )
+
+    def landed(slot, sem):
+        pltpu.make_async_copy(slot, slot, sem).wait()
+
+    def mult(value, of):
+        return pl.multiple_of(value, of)
+
+    loads = [
+        pltpu.make_async_copy(
+            kv_hbm.at[:, pl.ds(g * 2 * HEAD_DIM, 2 * HEAD_DIM)], kvs.at[tok, g], load_sem.at[g]
+        )
+        for g in range(kv_groups)
+    ]
+    bulk = [
+        pltpu.make_async_copy(src, dst, load_sem.at[kv_groups + i])
+        for i, (src, dst) in enumerate(
+            [
+                (query_hbm, query_v),
+                (residual_hbm, residual_v),
+                (project_hbm, project_w),
+                (down_hbm, down_v),
+                (gate_hbm, gate_w),
+            ]
+        )
+    ]
+    for load in loads + bulk:
+        load.start()
+
+    barrier = pltpu.get_barrier_semaphore()
+
+    @pl.when(z > 0)
+    def _():
+        pl.semaphore_signal(barrier, 1, device_id=below, device_id_type=MESH_ID)
+
+    @pl.when(z < last)
+    def _():
+        pl.semaphore_signal(barrier, 1, device_id=above, device_id_type=MESH_ID)
+
+    pl.semaphore_signal(barrier, 1, device_id=other, device_id_type=MESH_ID)
+    pl.semaphore_signal(barrier, 1, device_id=peer, device_id_type=MESH_ID)
+    sides = jnp.where(z > 0, 1, 0) + jnp.where(z < last, 1, 0)
+    pl.semaphore_wait(barrier, sides + 2)
+
+    def kv_up(chip):
+        slot = kvs.at[chip * cores + c]
+        return remote(slot, slot, kv_up_send.at[chip], kv_recv.at[chip, c], above)
+
+    def kv_core(chip):
+        slot = kvs.at[chip * cores + c]
+        return remote(slot, slot, kv_core_send.at[chip], kv_recv.at[chip, c], other)
+
+    def kv_wait(chip, core):
+        landed(kvs.at[chip * cores + core], kv_recv.at[chip, core])
+
+    def kv_pass(chip):
+        @pl.when(z < last)
+        def _():
+            kv_up(chip).start()
+
+        kv_core(chip).start()
+
+    for load in loads:
+        load.wait()
+    kv_pass(z)
+
+    bulk[0].wait()
+    for g in range(kv_groups):
+        query_t[g, HEAD_DIM:, :] = jnp.zeros((HEAD_DIM, repeat * depth), bf16)
+        for m in range(repeat // 2):
+            lane = (g * repeat + 2 * m) * HEAD_DIM
+            turned = (query_v[:, lane:lane + 2 * HEAD_DIM].astype(f32) * 0.125).T.astype(bf16)
+            query_t[g, :HEAD_DIM, 2 * m * depth:(2 * m + 1) * depth] = turned[:HEAD_DIM]
+            query_t[g, :HEAD_DIM, (2 * m + 1) * depth:(2 * m + 2) * depth] = turned[HEAD_DIM:]
+        for r in range(repeat):
+            row_max[g, :, r * depth:(r + 1) * depth] = jnp.full(
+                (1, depth), sink_ref[g * repeat + r], f32
+            )
+    row_total[...] = jnp.ones(row_total.shape, f32)
+    accum[...] = jnp.zeros(accum.shape, f32)
+
+    def attend(chip, g, masked):
+        keys = kvs[pl.ds(chip * cores, cores), g].reshape(cores * depth, 2 * HEAD_DIM)
+        values = keys.astype(f32).T[HEAD_DIM:].astype(bf16)
+        for m in range(repeat // 2):
+            lanes = slice(2 * m * depth, (2 * m + 2) * depth)
+            scores = jnp.dot(keys, query_t[g, :, lanes], preferred_element_type=f32)
+            if masked:
+                row = lax.broadcasted_iota(jnp.int32, scores.shape, 0)
+                column = lax.broadcasted_iota(jnp.int32, scores.shape, 1)
+                column = jnp.where(column >= depth, column - depth, column)
+                scores = jnp.where(row <= c * depth + column, scores, jnp.float32(-1e30))
+            old = row_max[g, :, lanes]
+            new = jnp.maximum(old, jnp.max(scores, axis=0, keepdims=True))
+            weights = jnp.exp(scores - new)
+            decay = jnp.exp(old - new)
+            row_max[g, :, lanes] = new
+            row_total[g, :, lanes] = row_total[g, :, lanes] * decay + jnp.sum(
+                weights, axis=0, keepdims=True
+            )
+            accum[g, :, lanes] = accum[g, :, lanes] * decay + jnp.dot(
+                values, weights.astype(bf16), preferred_element_type=f32
+            )
+
+    def attend_chip(chip, masked):
+        kv_wait(chip, 1 - c)
+
+        def group(g, carry):
+            attend(chip, g, masked)
+            return carry
+
+        lax.fori_loop(0, kv_groups // 2, group, 0)
+
+        @pl.when(chip > 0)
+        def _():
+            kv_wait(chip - 1, c)
+            kv_pass(chip - 1)
+
+        lax.fori_loop(kv_groups // 2, kv_groups, group, 0)
+
+    attend_chip(z, True)
+
+    def earlier(i, carry):
+        attend_chip(z - i, False)
+        return carry
+
+    lax.fori_loop(1, z + 1, earlier, 0)
+
+    for g in range(kv_groups):
+        inverse = 1.0 / row_total[g]
+        for r in range(repeat):
+            lanes = slice(r * depth, (r + 1) * depth)
+            head = (g * repeat + r) * HEAD_DIM
+            attended[head:head + HEAD_DIM, :] = (accum[g, :, lanes] * inverse[:, lanes]).astype(bf16)
+
+    order = [side * own + k for k in range(own) for side in range(2)]
+    order += list(range(2 * own, full + (1 if tail else 0)))
+    spans = {k: (k * chunk, tail if k == full else chunk) for k in order}
+
+    def parts_copy(k):
+        start, size = spans[k]
+        return remote(
+            parts.at[pl.ds(start, size)], peer_parts.at[pl.ds(start, size)],
+            parts_send.at[k], parts_recv.at[k], peer,
+        )
+
+    bulk[1].wait()
+    bulk[2].wait()
+    for k in order:
+        start, size = spans[k]
+        block = slice(start, start + size)
+        value = jnp.dot(project_w[block, :], attended[...], preferred_element_type=f32)
+        parts[block, :] = value.astype(bf16)
+        parts_copy(k).start()
+        stream[block, :] = value + residual_v[block, :].astype(f32)
+
+    lanes_all = -(-width // 128)
+    for b in range(lanes_all):
+        size = min(128, width - b * 128)
+        gain = gain_ref[:, b * 128:b * 128 + size]
+        gain_cols[b * 128:b * 128 + size, :] = jnp.broadcast_to(gain, (128, size)).T
+
+    bulk[3].wait()
+
+    def turn(b, carry):
+        at = pl.ds(mult(b * 128, 128), 128)
+        down_t[at, :] = down_v[:, at].astype(f32).T.astype(bf16)
+        return carry
+
+    lax.fori_loop(0, width // 128, turn, 0)
+    if width % 128:
+        at = pl.ds(width // 128 * 128, width % 128)
+        down_t[at, :] = down_v[:, at].astype(f32).T.astype(bf16)
+
+    def carried(k):
+        return k >= 2 * own
+
+    def row_slot(chip, core, start, size):
+        return rows.at[chip, core, pl.ds(start, size)]
+
+    def row_copy(chip, k, size, send, target):
+        slot = row_slot(chip, c, mult(k * chunk, chunk), size)
+        return remote(slot, slot, send.at[chip, k], row_recv.at[chip, c, k], target)
+
+    def row_wait(chip, core, k, size):
+        landed(row_slot(chip, core, mult(k * chunk, chunk), size), row_recv.at[chip, core, k])
+
+    def pass_along(chip, k, size):
+        @pl.when((chip <= z) & (z < last))
+        def _():
+            row_copy(chip, k, size, row_up, above).start()
+
+        @pl.when((chip >= z) & (z > 0))
+        def _():
+            row_copy(chip, k, size, row_down, below).start()
+
+    def meta_copy(chip, send, target):
+        slot = meta.at[chip, c]
+        return remote(slot, slot, send.at[chip], meta_recv.at[chip, c], target)
+
+    def meta_wait(chip, core):
+        landed(meta.at[chip, core], meta_recv.at[chip, core])
+
+    def pass_meta(chip):
+        @pl.when((chip <= z) & (z < last))
+        def _():
+            meta_copy(chip, meta_up, above).start()
+
+        @pl.when((chip >= z) & (z > 0))
+        def _():
+            meta_copy(chip, meta_down, below).start()
+
+        meta_copy(chip, meta_core, other).start()
+
+    squares = jnp.zeros((8, depth), f32)
+    for k in order:
+        start, size = spans[k]
+        block = slice(start, start + size)
+        landed(peer_parts.at[pl.ds(start, size)], parts_recv.at[k])
+        value = stream[block, :] + peer_parts[block, :].astype(f32)
+        stream[block, :] = value
+        rows[z, c, block, :] = (value * gain_cols[block, :]).astype(bf16)
+        squares += jnp.sum((value * value).reshape(size // 8, 8, depth), axis=0)
+        if carried(k):
+            pass_along(z, k, size)
+        else:
+            @pl.when(x == k // own)
+            def _():
+                pass_along(z, k, size)
+
+        row_copy(z, k, size, row_core, other).start()
+    total = jnp.sum(squares, axis=0, keepdims=True)
+    scale = lax.rsqrt(total / width + 1e-05)
+    meta[z, c, 0:8, :] = jnp.broadcast_to(scale, (8, depth))
+    experts = chips * cores
+    expert = lax.broadcasted_iota(jnp.int32, (experts, depth), 0)
+    dense = jnp.zeros((experts, depth), f32)
+    for k in range(ids_ref.shape[0]):
+        dense += jnp.where(ids_ref[k:k + 1, :] == expert, route_ref[k:k + 1, :], 0.0)
+    meta[z, c, pl.ds(8, experts), :] = dense
+    pass_meta(z)
+
+    bulk[4].wait()
+
+    near = jnp.minimum(z, last - z)
+
+    def chip_at(i):
+        inner = jnp.where(i % 2 == 1, z - (i + 1) // 2, z + i // 2)
+        outer = jnp.where(z < last - z, i, last - i)
+        return jnp.where(i <= 2 * near, inner, outer)
+
+    def each_side(i, act):
+        @pl.when(z - 1 - i >= 0)
+        def _():
+            act(z - 1 - i)
+
+        @pl.when(z + 1 + i <= last)
+        def _():
+            act(z + 1 + i)
+
+    def pump_line(i, k, size, crosses):
+        def act(chip):
+            row_wait(chip, c, k, size)
+            pass_along(chip, k, size)
+            if crosses is not None:
+                @pl.when(crosses)
+                def _():
+                    row_copy(chip, k, size, row_peer, peer).start()
+
+            row_copy(chip, k, size, row_core, other).start()
+
+        each_side(i, act)
+
+    def pump_cross(i, k, size):
+        def act(chip):
+            row_wait(chip, c, k, size)
+            row_copy(chip, k, size, row_core, other).start()
+
+        each_side(i, act)
+
+    def multiply(chip, k, size):
+        row_wait(chip, 1 - c, k, size)
+        at = pl.ds(mult(k * chunk, chunk), size)
+        both = jnp.concatenate([rows[chip, c, at, :], rows[chip, 1 - c, at, :]], axis=1)
+        for side in range(2):
+            hidden[side] += jnp.dot(gate_w[side, :, at], both, preferred_element_type=f32)
+
+    def part_copy(chip, r):
+        return remote(
+            part.at[chip, r], from_core.at[chip, r], part_send.at[chip, r],
+            part_recv.at[chip, r], other,
+        )
+
+    def cross_copy(chip, r):
+        return remote(
+            cross.at[chip, r], from_peer.at[chip, r], peer_send.at[chip, r],
+            peer_recv.at[chip, r], peer,
+        )
+
+    def up_hop(chip, r):
+        return remote(
+            hop.at[chip, r], from_left.at[chip, r], hop_send.at[chip, r],
+            left_recv.at[chip, r], above,
+        )
+
+    def down_hop(chip, r):
+        return remote(
+            hop.at[chip, r], from_right.at[chip, r], hop_send.at[chip, r],
+            right_recv.at[chip, r], below,
+        )
+
+
+    def send_sum(chip, incoming, buffer, sem, copy):
+        def one(r, carry):
+            landed(from_peer.at[chip, r], peer_recv.at[chip, r])
+            value = kept[chip, x * pieces + r].astype(f32) + from_peer[chip, r].astype(f32)
+
+            @pl.when(incoming)
+            def _():
+                landed(buffer.at[chip, r], sem.at[chip, r])
+                hop[chip, r] = (value + buffer[chip, r].astype(f32)).astype(bf16)
+
+            @pl.when(jnp.logical_not(incoming))
+            def _():
+                hop[chip, r] = value.astype(bf16)
+
+            copy(chip, r).start()
+            return carry
+
+        lax.fori_loop(0, pieces, one, 0)
+
+    def step(i, carry):
+        chip = chip_at(i)
+        hidden[...] = jnp.zeros(hidden.shape, f32)
+
+        def line(t, carry):
+            k = jnp.where(t < own, own * x + t, own + t)
+            pump_line(i, k, chunk, t < own)
+            multiply(chip, k, chunk)
+            return carry
+
+        lax.fori_loop(0, own + shared, line, 0)
+        if tail:
+            pump_line(i, full, tail, None)
+            multiply(chip, full, tail)
+
+        def forward_meta(q):
+            meta_wait(q, c)
+            pass_meta(q)
+
+        each_side(i, forward_meta)
+
+        def crossed(t, carry):
+            k = own * (1 - x) + t
+            pump_cross(i, k, chunk)
+            multiply(chip, k, chunk)
+            return carry
+
+        lax.fori_loop(0, own, crossed, 0)
+
+        meta_wait(chip, 1 - c)
+        scale = jnp.concatenate([meta[chip, c, 0:1, :], meta[chip, 1 - c, 0:1, :]], axis=1)
+        weight = jnp.concatenate(
+            [meta[chip, c, pl.ds(8 + tok, 1), :], meta[chip, 1 - c, pl.ds(8 + tok, 1), :]], axis=1
+        )
+        gate = hidden[0] * scale
+        up = hidden[1] * scale
+        active[...] = (gate * jax.nn.sigmoid(1.702 * gate) * (up + 1.0) * weight).astype(bf16)
+
+        def spread(r, carry):
+            at = jnp.where(r < pieces, (1 - x) * pieces + r, x * pieces + r - pieces)
+            value = jnp.dot(
+                down_t[pl.ds(mult(at * piece, piece), piece), :], active[...],
+                preferred_element_type=f32,
+            )
+            part[chip, at] = value[:, depth:].astype(bf16)
+            part_copy(chip, at).start()
+            kept[chip, at] = value[:, :depth].astype(bf16)
+            return carry
+
+        lax.fori_loop(0, 2 * pieces, spread, 0)
+
+        def join(r, carry):
+            at = (1 - x) * pieces + r
+            landed(from_core.at[chip, at], part_recv.at[chip, at])
+            value = kept[chip, at].astype(f32) + from_core[chip, at].astype(f32)
+            cross[chip, r] = value.astype(bf16)
+            cross_copy(chip, r).start()
+            return carry
+
+        lax.fori_loop(0, pieces, join, 0)
+
+        def keep(r, carry):
+            at = x * pieces + r
+            landed(from_core.at[chip, at], part_recv.at[chip, at])
+            value = kept[chip, at].astype(f32) + from_core[chip, at].astype(f32)
+            kept[chip, at] = value.astype(bf16)
+            return carry
+
+        lax.fori_loop(0, pieces, keep, 0)
+
+        @pl.when(i > z)
+        def _():
+            send_sum(i, z > 0, from_left, left_recv, up_hop)
+
+        @pl.when((i > 0) & (last - i < z))
+        def _():
+            send_sum(last - i, z < last, from_right, right_recv, down_hop)
+
+        return carry
+
+    lax.fori_loop(0, chips, step, 0)
+
+    def finish(r, carry):
+        at = pl.ds(mult(x * half + r * piece, 16), piece)
+        landed(from_peer.at[z, r], peer_recv.at[z, r])
+        stream[at, :] += (
+            kept[z, x * pieces + r].astype(f32) + from_peer[z, r].astype(f32)
+        )
+
+        @pl.when(z > 0)
+        def _():
+            landed(from_left.at[z, r], left_recv.at[z, r])
+            stream[at, :] += from_left[z, r].astype(f32)
+
+        @pl.when(z < last)
+        def _():
+            landed(from_right.at[z, r], right_recv.at[z, r])
+            stream[at, :] += from_right[z, r].astype(f32)
+
+        out_ref[pl.ds(mult(r * piece, piece), piece), :] = stream[at, :].astype(bf16)
+        return carry
+
+    lax.fori_loop(0, pieces, finish, 0)
+
+    def drain(chip, carry):
+        @pl.when(chip <= z)
+        def _():
+            kv_core(chip).wait_send()
+
+        @pl.when((chip <= z) & (z < last))
+        def _():
+            kv_up(chip).wait_send()
+
+        def sent(k, size, on_line, crosses):
+            def line():
+                @pl.when((chip <= z) & (z < last))
+                def _():
+                    row_copy(chip, k, size, row_up, above).wait_send()
+
+                @pl.when((chip >= z) & (z > 0))
+                def _():
+                    row_copy(chip, k, size, row_down, below).wait_send()
+
+            if on_line:
+                line()
+            if crosses:
+                @pl.when(chip != z)
+                def _():
+                    row_copy(chip, k, size, row_peer, peer).wait_send()
+
+            row_copy(chip, k, size, row_core, other).wait_send()
+
+        for t in range(own):
+            sent(own * x + t, chunk, True, True)
+            sent(own * (1 - x) + t, chunk, False, False)
+        for t in range(shared):
+            sent(2 * own + t, chunk, True, False)
+        if tail:
+            sent(full, tail, True, False)
+
+        @pl.when((chip <= z) & (z < last))
+        def _():
+            meta_copy(chip, meta_up, above).wait_send()
+
+        @pl.when((chip >= z) & (z > 0))
+        def _():
+            meta_copy(chip, meta_down, below).wait_send()
+
+        meta_copy(chip, meta_core, other).wait_send()
+        for r in range(2 * pieces):
+            part_copy(chip, r).wait_send()
+        for r in range(pieces):
+            cross_copy(chip, r).wait_send()
+
+            @pl.when(chip > z)
+            def _():
+                up_hop(chip, r).wait_send()
+
+            @pl.when(chip < z)
+            def _():
+                down_hop(chip, r).wait_send()
+
+        return carry
+
+    lax.fori_loop(0, chips, drain, 0)
+    for k in order:
+        parts_copy(k).wait_send()
+
+
+def whole_layer(
+    dims, sinks, ids, route, gain, queries, keys_values, residual, project, gate_up, down
+):
+    chips, pairs, chunk, piece = dims
+    cores = 2
+    width, depth = residual.shape
+    kv_groups = keys_values.shape[1] // (2 * HEAD_DIM)
+    heads = queries.shape[1] // HEAD_DIM
+    repeat = heads // kv_groups
+    hidden = down.shape[0]
+    half = width // 2
+    pieces = half // piece
+    count = -(-width // chunk)
+    bf16, f32 = jnp.bfloat16, jnp.float32
+    dma = pltpu.SemaphoreType.DMA
+    vmem = pltpu.VMEM
+    experts = chips * cores
+    flops = 2 * width * (
+        depth * heads * HEAD_DIM + chips * cores * depth * 3 * hidden
+    )
+    return pl.pallas_call(
+        functools.partial(layer_kernel, dims),
+        out_shape=jax.ShapeDtypeStruct((half, depth), bf16),
+        in_specs=[pl.BlockSpec(memory_space=pltpu.SMEM)]
+        + [pl.BlockSpec(memory_space=pltpu.VMEM)] * 3
+        + [pl.BlockSpec(memory_space=pl.ANY)] * 6,
+        out_specs=pl.BlockSpec(memory_space=pltpu.VMEM),
+        scratch_shapes=[
+            vmem(queries.shape, bf16),
+            vmem((kv_groups, 2 * HEAD_DIM, repeat * depth), bf16),
+            vmem((experts, kv_groups, depth, 2 * HEAD_DIM), bf16),
+            vmem((kv_groups, 1, repeat * depth), f32),
+            vmem((kv_groups, 1, repeat * depth), f32),
+            vmem((kv_groups, HEAD_DIM, repeat * depth), f32),
+            vmem((heads * HEAD_DIM, depth), bf16),
+            vmem(residual.shape, bf16),
+            vmem(project.shape, bf16),
+            vmem(gate_up.shape, bf16),
+            vmem(down.shape, bf16),
+            vmem((width, hidden), bf16),
+            vmem((width, depth), f32),
+            vmem((width, depth), f32),
+            vmem((width, depth), bf16),
+            vmem((width, depth), bf16),
+            vmem((chips, cores, width, depth), bf16),
+            vmem((chips, cores, 8 + experts, depth), f32),
+            vmem((2, hidden, cores * depth), f32),
+            vmem((hidden, cores * depth), bf16),
+            vmem((chips, 2 * pieces, piece, depth), bf16),
+            vmem((chips, 2 * pieces, piece, depth), bf16),
+            vmem((chips, 2 * pieces, piece, depth), bf16),
+            vmem((chips, pieces, piece, depth), bf16),
+            vmem((chips, pieces, piece, depth), bf16),
+            vmem((chips, pieces, piece, depth), bf16),
+            vmem((chips, pieces, piece, depth), bf16),
+            vmem((chips, pieces, piece, depth), bf16),
+            dma((kv_groups + 5,)),
+            dma((chips, cores)),
+            dma((chips,)),
+            dma((chips,)),
+            dma((count,)),
+            dma((count,)),
+            dma((chips, cores, count)),
+            dma((chips, count)),
+            dma((chips, count)),
+            dma((chips, count)),
+            dma((chips, count)),
+            dma((chips, cores)),
+            dma((chips,)),
+            dma((chips,)),
+            dma((chips,)),
+            dma((chips, 2 * pieces)),
+            dma((chips, 2 * pieces)),
+            dma((chips, pieces)),
+            dma((chips, pieces)),
+            dma((chips, pieces)),
+            dma((chips, pieces)),
+            dma((chips, pieces)),
+        ],
+        compiler_params=pltpu.CompilerParams(
+            collective_id=0, has_side_effects=True, vmem_limit_bytes=VMEM_BYTES
+        ),
+        cost_estimate=pl.CostEstimate(
+            flops=flops,
+            bytes_accessed=2 * (project.size + gate_up.size + down.size),
+            transcendentals=0,
+        ),
+    )(sinks, ids, route, gain, queries, keys_values, residual, project, gate_up, down)
+
+
+def per_device_whole(
+    queries,
+    keys_values,
+    sink_logits,
+    residual,
+    out_weight,
+    norm_gain,
+    expert_ids,
+    route_weights,
+    gate_up,
+    down_weight,
+):
+    width = residual.shape[1]
+    pairs = lax.axis_size("pair")
+    chips = lax.axis_size("tok") // 2
+    half = width // 2
+    chunk = min(512, half // 128 * 128)
+    piece = next(n for n in (480, 240, 160, 80, 48, 32, 16, half) if half % n == 0)
+    out = whole_layer(
+        (chips, pairs, chunk, piece),
+        sink_logits,
+        expert_ids.T,
+        route_weights.T,
+        norm_gain[None, :],
+        queries,
+        keys_values,
+        residual.T,
+        out_weight.T,
+        jnp.transpose(gate_up[0], (1, 2, 0)),
+        down_weight[0],
+    )
+    return out.T
+
+
 def solution(mesh):
     placed = (
         P(("groups", "tok"), ("head", "pair")),
@@ -504,8 +1221,10 @@
         P("tok", None, None, ("head", "pair")),
         P("tok", ("head", "pair"), None),
     )
+    sizes = mesh.shape
+    chip_pair = sizes["pair"] == 1 and sizes["head"] == 2 and sizes["tok"] % 2 == 0
     return jax.shard_map(
-        per_device,
+        per_device_whole if chip_pair else per_device,
         mesh=mesh,
         in_specs=placed,
         out_specs=P(("groups", "tok"), ("head", "pair")),

time: 194 us -> 136 us (0.70)
  local copies, waits for them, and re-layouts: 33.9 us -> 3.06 us
  matrix products: 19.5 us -> 0 us
  Pallas kernels: 117 us -> 133 us
  between operations: 13.6 us -> 0.01 us
  other arithmetic: 9.44 us -> 0 us
    dot_general x3 -> x0, matrix products: 19.5 us -> none  [the longest x1 8.16 us: per_device(): jnp.einsum('tgrd,ngd->grtn', grouped, split_piece[:, :, 0], preferred_ele...]
    pallas_call x1, Pallas kernels: 117 us -> 133 us  [whole_layer(): pl.pallas_call(functools.partial(layer_kernel, dims), out_shape=jax.Shape...]
    transpose x1 -> x0, local copies, waits for them, and re-layouts: 12 us -> none  [per_device(): jnp.transpose(gate_up[0], (1, 0, 2)).reshape(2, shares, share, hidden)]
    reduce_sum x2 -> x0, other arithmetic: 9.18 us -> none  [the longest x1 9.17 us: per_device(): totals = totals * decay + jnp.sum(weights, axis=-1)]
    unnamed x26 -> x1, local copies, waits for them, and re-layouts: 9.74 us -> 1.75 us
    another operation x1 -> x0, local copies, waits for them, and re-layouts: 6.54 us -> none  [per_device(): down_weight[0].reshape(hidden, shares, share)]
    pad x4 -> x0, local copies, waits for them, and re-layouts: 2.58 us -> none  [the longest x1 0.95 us: per_device(): parts = jnp.pad(parts, ((0, 0), (0, 0), spare))]
  transfers between devices with their start and end apart: 1 -> 0, of which waited for: 0 -> 0; matrix products, arithmetic and copies ran while one was open for 15% -> 0% of each run, Pallas kernels for 0% -> 0%
where the time goes in v1:
time: 136 us
  Pallas kernels  133 us (98%)
  local copies, waits for them, and re-layouts  3.06 us (2%)
    pallas_call x1, Pallas kernels, whole_layer(): pl.pallas_call(functools.partial(layer_kernel, dims), out_shape=jax.Shape...  133 us

profile of v1, /device:TPU:0, one launch (start us, length us, event | category | flops | bytes accessed | tf_op | source)
XLA Modules:
  0.0 135.7 jit_solution(7987620595943723734)
XLA Ops:
  0.0 1.3 broadcast_in_dim.3.gain_ref
  1.3 132.6 %shard_map.100 = bf16[1440,128]{1,0:T(8,128)(2,1)} custom-call(f32[32]{0:T(128)} %sink_ref.1, s32[4,128]{1,0:T(4,128)} %bitcast.14, f32[4,128]{1,0:T(4,128)} %bitcast.15, f32[1,2880]{1,0:T(1,128)} %broadcast_in_dim.3.gain_ref, bf16[128,2048]{1,0:T(8,128)(2,1)} %query_hbm.1, bf16[128,512]{1,0:T(8,128)(2,1)} %kv_hbm.1, bf16[2880,128]{1,0:T(8,128)(2,1)} %bitcast.13, ...), custom_call_target="tpu_custom_call" | custom-call | flops 14250147840 | bytes 24238080 | tf_op jit(solution)/shard_map/pallas_call | solution.py:1107
  133.9 1.7 %copy.12 = bf16[128,1440]{0,1:T(8,128)(2,1)} copy(bf16[128,1440]{0,1:T(8,128)(2,1)} %bitcast.9) | data formatting | bytes 737280

commit v2 on v1

--- a/solution.py
+++ b/solution.py
@@ -12,6 +12,8 @@
 MESH_ID = pl.DeviceIdType.MESH
 
 VMEM_BYTES = 67_043_328
+OWN_LESS = 0
+BOTH = 1
 
 
 def moe_kernel(
@@ -532,14 +534,19 @@
     cross,
     from_peer,
     hop,
-    from_left,
-    from_right,
+    inbox,
+    closing,
+    from_closing,
+    acc,
+    squares,
+    peer_squares,
     load_sem,
     kv_recv,
     kv_core_send,
     kv_up_send,
     parts_send,
     parts_recv,
+    squares_sem,
     row_recv,
     row_up,
     row_down,
@@ -554,20 +561,22 @@
     peer_send,
     peer_recv,
     hop_send,
-    left_recv,
-    right_recv,
+    inbox_recv,
+    closing_send,
+    closing_recv,
 ):
-    chips, pairs, chunk, piece = dims
+    chips, pairs, chunk, piece, own, both = dims
     cores = 2
     width, depth = residual_hbm.shape
     kv_groups = kvs.shape[1]
     repeat = query_t.shape[2] // depth
     half = width // 2
     f32, bf16 = jnp.float32, jnp.bfloat16
-    full = width // chunk
-    tail = width - full * chunk
-    own = full // 2
-    shared = full - 2 * own
+    far = (width - own * chunk) // 128 * 128
+    edges = [(at, min(chunk, far - at)) for at in range(own * chunk, far, chunk)]
+    if far + own * chunk < width:
+        edges.append((far + own * chunk, width - far - own * chunk))
+    spread_over = [(2 * own + n, at, size) for n, (at, size) in enumerate(edges)]
     pieces = half // piece
     last = chips - 1
 
@@ -649,6 +658,11 @@
     for load in loads:
         load.wait()
     kv_pass(z)
+
+    for b in range(-(-width // 128)):
+        size = min(128, width - b * 128)
+        gain = gain_ref[:, b * 128:b * 128 + size]
+        gain_cols[b * 128:b * 128 + size, :] = jnp.broadcast_to(gain, (128, size)).T
 
     bulk[0].wait()
     for g in range(kv_groups):
@@ -668,25 +682,32 @@
     def attend(chip, g, masked):
         keys = kvs[pl.ds(chip * cores, cores), g].reshape(cores * depth, 2 * HEAD_DIM)
         values = keys.astype(f32).T[HEAD_DIM:].astype(bf16)
-        for m in range(repeat // 2):
-            lanes = slice(2 * m * depth, (2 * m + 2) * depth)
-            scores = jnp.dot(keys, query_t[g, :, lanes], preferred_element_type=f32)
-            if masked:
-                row = lax.broadcasted_iota(jnp.int32, scores.shape, 0)
-                column = lax.broadcasted_iota(jnp.int32, scores.shape, 1)
-                column = jnp.where(column >= depth, column - depth, column)
-                scores = jnp.where(row <= c * depth + column, scores, jnp.float32(-1e30))
-            old = row_max[g, :, lanes]
-            new = jnp.maximum(old, jnp.max(scores, axis=0, keepdims=True))
-            weights = jnp.exp(scores - new)
-            decay = jnp.exp(old - new)
-            row_max[g, :, lanes] = new
-            row_total[g, :, lanes] = row_total[g, :, lanes] * decay + jnp.sum(
-                weights, axis=0, keepdims=True
+        olds, totals, sums = row_max[g], row_total[g], accum[g]
+        lanes = [slice(2 * m * depth, (2 * m + 2) * depth) for m in range(repeat // 2)]
+        scores = [
+            jnp.dot(keys, query_t[g, :, lane], preferred_element_type=f32) for lane in lanes
+        ]
+        if masked:
+            row = lax.broadcasted_iota(jnp.int32, scores[0].shape, 0)
+            column = lax.broadcasted_iota(jnp.int32, scores[0].shape, 1)
+            column = jnp.where(column >= depth, column - depth, column)
+            allowed = row <= c * depth + column
+            scores = [jnp.where(allowed, score, jnp.float32(-1e30)) for score in scores]
+        news = [
+            jnp.maximum(olds[:, lane], jnp.max(score, axis=0, keepdims=True))
+            for lane, score in zip(lanes, scores)
+        ]
+        weights = [jnp.exp(score - new) for score, new in zip(scores, news)]
+        added = [
+            jnp.dot(values, weight.astype(bf16), preferred_element_type=f32) for weight in weights
+        ]
+        for lane, new, weight, more in zip(lanes, news, weights, added):
+            decay = jnp.exp(olds[:, lane] - new)
+            row_max[g, :, lane] = new
+            row_total[g, :, lane] = totals[:, lane] * decay + jnp.sum(
+                weight, axis=0, keepdims=True
             )
-            accum[g, :, lanes] = accum[g, :, lanes] * decay + jnp.dot(
-                values, weights.astype(bf16), preferred_element_type=f32
-            )
+            accum[g, :, lane] = sums[:, lane] * decay + more
 
     def attend_chip(chip, masked):
         kv_wait(chip, 1 - c)
@@ -719,66 +740,48 @@
             head = (g * repeat + r) * HEAD_DIM
             attended[head:head + HEAD_DIM, :] = (accum[g, :, lanes] * inverse[:, lanes]).astype(bf16)
 
-    order = [side * own + k for k in range(own) for side in range(2)]
-    order += list(range(2 * own, full + (1 if tail else 0)))
-    spans = {k: (k * chunk, tail if k == full else chunk) for k in order}
-
-    def parts_copy(k):
-        start, size = spans[k]
+    def own_at(side, t):
+        return mult(side * far + t * chunk, 128)
+
+    def own_id(side, t):
+        return side * own + t
+
+    def parts_copy(n, start, size):
         return remote(
             parts.at[pl.ds(start, size)], peer_parts.at[pl.ds(start, size)],
-            parts_send.at[k], parts_recv.at[k], peer,
-        )
-
-    bulk[1].wait()
-    bulk[2].wait()
-    for k in order:
-        start, size = spans[k]
-        block = slice(start, start + size)
-        value = jnp.dot(project_w[block, :], attended[...], preferred_element_type=f32)
-        parts[block, :] = value.astype(bf16)
-        parts_copy(k).start()
-        stream[block, :] = value + residual_v[block, :].astype(f32)
-
-    lanes_all = -(-width // 128)
-    for b in range(lanes_all):
-        size = min(128, width - b * 128)
-        gain = gain_ref[:, b * 128:b * 128 + size]
-        gain_cols[b * 128:b * 128 + size, :] = jnp.broadcast_to(gain, (128, size)).T
-
-    bulk[3].wait()
-
-    def turn(b, carry):
-        at = pl.ds(mult(b * 128, 128), 128)
-        down_t[at, :] = down_v[:, at].astype(f32).T.astype(bf16)
-        return carry
-
-    lax.fori_loop(0, width // 128, turn, 0)
-    if width % 128:
-        at = pl.ds(width // 128 * 128, width % 128)
-        down_t[at, :] = down_v[:, at].astype(f32).T.astype(bf16)
-
-    def carried(k):
-        return k >= 2 * own
-
-    def row_slot(chip, core, start, size):
-        return rows.at[chip, core, pl.ds(start, size)]
-
-    def row_copy(chip, k, size, send, target):
-        slot = row_slot(chip, c, mult(k * chunk, chunk), size)
+            parts_send.at[n], parts_recv.at[n], peer,
+        )
+
+    def project(start, size):
+        return jnp.dot(
+            project_w[pl.ds(start, size), :], attended[...], preferred_element_type=f32
+        )
+
+    def give(n, start, size):
+        value = project(start, size)
+        parts[pl.ds(start, size), :] = value.astype(bf16)
+        parts_copy(n, start, size).start()
+        return value
+
+    def hold(start, size, value):
+        at = pl.ds(start, size)
+        stream[at, :] = value + residual_v[at, :].astype(f32)
+
+    def row_copy(chip, k, start, size, send, target):
+        slot = rows.at[chip, c, pl.ds(start, size)]
         return remote(slot, slot, send.at[chip, k], row_recv.at[chip, c, k], target)
 
-    def row_wait(chip, core, k, size):
-        landed(row_slot(chip, core, mult(k * chunk, chunk), size), row_recv.at[chip, core, k])
-
-    def pass_along(chip, k, size):
+    def row_wait(chip, core, k, start, size):
+        landed(rows.at[chip, core, pl.ds(start, size)], row_recv.at[chip, core, k])
+
+    def pass_along(chip, k, start, size):
         @pl.when((chip <= z) & (z < last))
         def _():
-            row_copy(chip, k, size, row_up, above).start()
+            row_copy(chip, k, start, size, row_up, above).start()
 
         @pl.when((chip >= z) & (z > 0))
         def _():
-            row_copy(chip, k, size, row_down, below).start()
+            row_copy(chip, k, start, size, row_down, below).start()
 
     def meta_copy(chip, send, target):
         slot = meta.at[chip, c]
@@ -798,35 +801,61 @@
 
         meta_copy(chip, meta_core, other).start()
 
-    squares = jnp.zeros((8, depth), f32)
-    for k in order:
-        start, size = spans[k]
-        block = slice(start, start + size)
-        landed(peer_parts.at[pl.ds(start, size)], parts_recv.at[k])
-        value = stream[block, :] + peer_parts[block, :].astype(f32)
-        stream[block, :] = value
-        rows[z, c, block, :] = (value * gain_cols[block, :]).astype(bf16)
-        squares += jnp.sum((value * value).reshape(size // 8, 8, depth), axis=0)
-        if carried(k):
-            pass_along(z, k, size)
-        else:
-            @pl.when(x == k // own)
-            def _():
-                pass_along(z, k, size)
-
-        row_copy(z, k, size, row_core, other).start()
-    total = jnp.sum(squares, axis=0, keepdims=True)
-    scale = lax.rsqrt(total / width + 1e-05)
-    meta[z, c, 0:8, :] = jnp.broadcast_to(scale, (8, depth))
+    def settle(n, k, start, size):
+        at = pl.ds(start, size)
+        landed(peer_parts.at[at], parts_recv.at[n])
+        value = stream[at, :] + peer_parts[at, :].astype(f32)
+        stream[at, :] = value
+        rows[z, c, at, :] = (value * gain_cols[at, :]).astype(bf16)
+        pass_along(z, k, start, size)
+        row_copy(z, k, start, size, row_core, other).start()
+        return jnp.sum((value * value).reshape(size // 8, 8, depth), axis=0)
+
+    bulk[1].wait()
+    bulk[2].wait()
+    for t in range(own):
+        give(t, own_at(1 - x, t), chunk)
+    squares_own = jnp.zeros((8, depth), f32)
+    squares_all = jnp.zeros((8, depth), f32)
+    for t in range(own):
+        hold(own_at(x, t), chunk, project(own_at(x, t), chunk))
+        for n, (k, start, size) in enumerate(spread_over):
+            if t == 0:
+                hold(start, size, give(own + n, start, size))
+        squares_own += settle(t, own_id(x, t), own_at(x, t), chunk)
+    squares[...] = squares_own
+    squares_copy = remote(squares, peer_squares, squares_sem.at[0], squares_sem.at[1], peer)
+    squares_copy.start()
+
     experts = chips * cores
     expert = lax.broadcasted_iota(jnp.int32, (experts, depth), 0)
     dense = jnp.zeros((experts, depth), f32)
     for k in range(ids_ref.shape[0]):
         dense += jnp.where(ids_ref[k:k + 1, :] == expert, route_ref[k:k + 1, :], 0.0)
     meta[z, c, pl.ds(8, experts), :] = dense
+    bulk[3].wait()
+
+    def turn(b, carry):
+        at = pl.ds(mult(b * 128, 128), 128)
+        down_t[at, :] = down_v[:, at].astype(f32).T.astype(bf16)
+        return carry
+
+    turns = width // 128
+    if width % 128:
+        at = pl.ds(turns * 128, width % 128)
+        down_t[at, :] = down_v[:, at].astype(f32).T.astype(bf16)
+    for n, (k, start, size) in enumerate(spread_over):
+        if n < 2:
+            lax.fori_loop(n * turns // 2, (n + 1) * turns // 2, turn, 0)
+        squares_all += settle(own + n, k, start, size)
+    if len(spread_over) < 2:
+        lax.fori_loop(len(spread_over) * turns // 2, turns, turn, 0)
+    landed(peer_squares, squares_sem.at[1])
+    squares_all += squares[...] + peer_squares[...]
+    total = jnp.sum(squares_all, axis=0, keepdims=True)
+    scale = lax.rsqrt(total / width + 1e-05)
+    meta[z, c, 0:8, :] = jnp.broadcast_to(scale, (8, depth))
     pass_meta(z)
-
-    bulk[4].wait()
 
     near = jnp.minimum(z, last - z)
 
@@ -844,32 +873,64 @@
         def _():
             act(z + 1 + i)
 
-    def pump_line(i, k, size, crosses):
+    def pump(i, k, start, size, crosses):
         def act(chip):
-            row_wait(chip, c, k, size)
-            pass_along(chip, k, size)
-            if crosses is not None:
-                @pl.when(crosses)
-                def _():
-                    row_copy(chip, k, size, row_peer, peer).start()
-
-            row_copy(chip, k, size, row_core, other).start()
+            row_wait(chip, c, k, start, size)
+            pass_along(chip, k, start, size)
+            if crosses:
+                row_copy(chip, k, start, size, row_peer, peer).start()
+            row_copy(chip, k, start, size, row_core, other).start()
 
         each_side(i, act)
 
-    def pump_cross(i, k, size):
+    def pump_all(i):
+        def one(t, carry):
+            pump(i, own_id(x, t), own_at(x, t), chunk, True)
+            return carry
+
+        lax.fori_loop(0, own, one, 0)
+        for k, start, size in spread_over:
+            pump(i, k, start, size, False)
+
         def act(chip):
-            row_wait(chip, c, k, size)
-            row_copy(chip, k, size, row_core, other).start()
+            meta_wait(chip, c)
+            pass_meta(chip)
 
         each_side(i, act)
 
-    def multiply(chip, k, size):
-        row_wait(chip, 1 - c, k, size)
-        at = pl.ds(mult(k * chunk, chunk), size)
-        both = jnp.concatenate([rows[chip, c, at, :], rows[chip, 1 - c, at, :]], axis=1)
+    def cross_in(chip):
+        def one(t, carry):
+            k, start = own_id(1 - x, t), own_at(1 - x, t)
+            row_wait(chip, c, k, start, chunk)
+            row_copy(chip, k, start, chunk, row_core, other).start()
+            return carry
+
+        lax.fori_loop(0, own, one, 0)
+
+    def multiply(chip, k, start, size):
+        row_wait(chip, 1 - c, k, start, size)
+        at = pl.ds(start, size)
+        pair = jnp.concatenate([rows[chip, c, at, :], rows[chip, 1 - c, at, :]], axis=1)
         for side in range(2):
-            hidden[side] += jnp.dot(gate_w[side, :, at], both, preferred_element_type=f32)
+            hidden[side] += jnp.dot(gate_w[side, :, at], pair, preferred_element_type=f32)
+
+    def multiply_line(chip):
+        hidden[...] = jnp.zeros(hidden.shape, f32)
+
+        def one(t, carry):
+            multiply(chip, own_id(x, t), own_at(x, t), chunk)
+            return carry
+
+        lax.fori_loop(0, own, one, 0)
+        for k, start, size in spread_over:
+            multiply(chip, k, start, size)
+
+    def multiply_crossed(chip):
+        def one(t, carry):
+            multiply(chip, own_id(1 - x, t), own_at(1 - x, t), chunk)
+            return carry
+
+        lax.fori_loop(0, own, one, 0)
 
     def part_copy(chip, r):
         return remote(
@@ -883,67 +944,62 @@
             peer_recv.at[chip, r], peer,
         )
 
-    def up_hop(chip, r):
+    def hop_copy(way, chip, u):
         return remote(
-            hop.at[chip, r], from_left.at[chip, r], hop_send.at[chip, r],
-            left_recv.at[chip, r], above,
-        )
-
-    def down_hop(chip, r):
+            hop.at[chip, u], inbox.at[way, chip, u], hop_send.at[chip, u],
+            inbox_recv.at[way, chip, u], {"tok": tok + cores * (1 - 2 * way)},
+        )
+
+    def last_copy(u):
         return remote(
-            hop.at[chip, r], from_right.at[chip, r], hop_send.at[chip, r],
-            right_recv.at[chip, r], below,
-        )
-
-
-    def send_sum(chip, incoming, buffer, sem, copy):
-        def one(r, carry):
-            landed(from_peer.at[chip, r], peer_recv.at[chip, r])
-            value = kept[chip, x * pieces + r].astype(f32) + from_peer[chip, r].astype(f32)
-
-            @pl.when(incoming)
+            closing.at[u], from_closing.at[u], closing_send.at[u], closing_recv.at[u], peer
+        )
+
+    def piece_of(u):
+        return jnp.where(u < both, (1 - x) * pieces + u, x * pieces + u - both)
+
+    slots = pieces + both
+    nearer = jnp.where(z < last - z, 0, 1)
+
+    def hops(i, ends):
+        def toward(turn_of, carry):
+            way = jnp.where(nearer == 0, turn_of, 1 - turn_of)
+            chip = jnp.where(way == 0, i, last - i)
+            incoming = jnp.where(way == 0, z, last - z) > 0
+            sends = jnp.where(way == 0, chip - z, z - chip) > 0
+            if ends is not None:
+                sends = sends & (incoming != ends)
+
+            def one(u, carry):
+                at = piece_of(u)
+                @pl.when(u >= 2 * both)
+                def _():
+                    r = jnp.maximum(u - 2 * both, 0)
+                    landed(from_peer.at[chip, r], peer_recv.at[chip, r])
+                    acc[...] = kept[chip, at].astype(f32) + from_peer[chip, r].astype(f32)
+
+                @pl.when(u < 2 * both)
+                def _():
+                    acc[...] = kept[chip, at].astype(f32)
+
+                @pl.when(incoming)
+                def _():
+                    landed(inbox.at[way, chip, u], inbox_recv.at[way, chip, u])
+                    acc[...] += inbox[way, chip, u].astype(f32)
+
+                hop[chip, u] = acc[...].astype(bf16)
+                hop_copy(way, chip, u).start()
+                return carry
+
+            @pl.when(sends)
             def _():
-                landed(buffer.at[chip, r], sem.at[chip, r])
-                hop[chip, r] = (value + buffer[chip, r].astype(f32)).astype(bf16)
-
-            @pl.when(jnp.logical_not(incoming))
-            def _():
-                hop[chip, r] = value.astype(bf16)
-
-            copy(chip, r).start()
+                lax.fori_loop(0, slots, one, 0)
+
             return carry
 
-        lax.fori_loop(0, pieces, one, 0)
-
-    def step(i, carry):
-        chip = chip_at(i)
-        hidden[...] = jnp.zeros(hidden.shape, f32)
-
-        def line(t, carry):
-            k = jnp.where(t < own, own * x + t, own + t)
-            pump_line(i, k, chunk, t < own)
-            multiply(chip, k, chunk)
-            return carry
-
-        lax.fori_loop(0, own + shared, line, 0)
-        if tail:
-            pump_line(i, full, tail, None)
-            multiply(chip, full, tail)
-
-        def forward_meta(q):
-            meta_wait(q, c)
-            pass_meta(q)
-
-        each_side(i, forward_meta)
-
-        def crossed(t, carry):
-            k = own * (1 - x) + t
-            pump_cross(i, k, chunk)
-            multiply(chip, k, chunk)
-            return carry
-
-        lax.fori_loop(0, own, crossed, 0)
-
+        lax.fori_loop(0, 2, toward, 0)
+
+    def finish_rows(chip, between=None):
         meta_wait(chip, 1 - c)
         scale = jnp.concatenate([meta[chip, c, 0:1, :], meta[chip, 1 - c, 0:1, :]], axis=1)
         weight = jnp.concatenate(
@@ -965,13 +1021,23 @@
             return carry
 
         lax.fori_loop(0, 2 * pieces, spread, 0)
+        if between is not None:
+            between()
 
         def join(r, carry):
             at = (1 - x) * pieces + r
             landed(from_core.at[chip, at], part_recv.at[chip, at])
             value = kept[chip, at].astype(f32) + from_core[chip, at].astype(f32)
-            cross[chip, r] = value.astype(bf16)
-            cross_copy(chip, r).start()
+
+            @pl.when(r >= both)
+            def _():
+                cross[chip, jnp.maximum(r - both, 0)] = value.astype(bf16)
+                cross_copy(chip, jnp.maximum(r - both, 0)).start()
+
+            @pl.when(r < both)
+            def _():
+                kept[chip, at] = value.astype(bf16)
+
             return carry
 
         lax.fori_loop(0, pieces, join, 0)
@@ -985,36 +1051,98 @@
 
         lax.fori_loop(0, pieces, keep, 0)
 
-        @pl.when(i > z)
-        def _():
-            send_sum(i, z > 0, from_left, left_recv, up_hop)
-
-        @pl.when((i > 0) & (last - i < z))
-        def _():
-            send_sum(last - i, z < last, from_right, right_recv, down_hop)
-
+    is_end = (z == 0) | (z == last)
+
+    def own_block():
+        multiply_line(z)
+        cross_in(z)
+        multiply_crossed(z)
+        finish_rows(z)
+
+    bulk[4].wait()
+    pump_all(0)
+
+    def step(i, carry):
+        chip = chip_at(i)
+        multiply_line(chip)
+        each_side(i - 1, cross_in)
+        multiply_crossed(chip)
+
+        @pl.when(jnp.logical_not(is_end))
+        def _():
+            pump_all(i)
+
+        @pl.when(i > 1)
+        def _():
+            hops(i - 1, True)
+
+        def between():
+            @pl.when(is_end)
+            def _():
+                pump_all(i)
+
+            @pl.when(i == jnp.where(is_end, last, 1))
+            def _():
+                for t in range(own):
+                    row_copy(z, own_id(x, t), own_at(x, t), chunk, row_peer, peer).start()
+
+        finish_rows(chip, between)
         return carry
 
-    lax.fori_loop(0, chips, step, 0)
+    lax.fori_loop(1, chips, step, 0)
+
+    @pl.when(jnp.logical_not(is_end))
+    def _():
+        own_block()
+
+    for i in range(1, last):
+        hops(i, False)
+    hops(last, None)
+
+    @pl.when(is_end)
+    def _():
+        own_block()
+
+    def from_line(u):
+        acc[...] = kept[z, piece_of(u)].astype(f32)
+
+        @pl.when(z > 0)
+        def _():
+            landed(inbox.at[0, z, u], inbox_recv.at[0, z, u])
+            acc[...] += inbox[0, z, u].astype(f32)
+
+        @pl.when(z < last)
+        def _():
+            landed(inbox.at[1, z, u], inbox_recv.at[1, z, u])
+            acc[...] += inbox[1, z, u].astype(f32)
+
+    def closes(u, carry):
+        from_line(u)
+        closing[u] = acc[...].astype(bf16)
+        last_copy(u).start()
+        return carry
+
+    lax.fori_loop(0, both, closes, 0)
 
     def finish(r, carry):
-        at = pl.ds(mult(x * half + r * piece, 16), piece)
-        landed(from_peer.at[z, r], peer_recv.at[z, r])
-        stream[at, :] += (
-            kept[z, x * pieces + r].astype(f32) + from_peer[z, r].astype(f32)
-        )
-
-        @pl.when(z > 0)
-        def _():
-            landed(from_left.at[z, r], left_recv.at[z, r])
-            stream[at, :] += from_left[z, r].astype(f32)
-
-        @pl.when(z < last)
-        def _():
-            landed(from_right.at[z, r], right_recv.at[z, r])
-            stream[at, :] += from_right[z, r].astype(f32)
-
-        out_ref[pl.ds(mult(r * piece, piece), piece), :] = stream[at, :].astype(bf16)
+        p = jnp.where(r < pieces - both, r + both, r - (pieces - both))
+        at = pl.ds(mult(x * half + p * piece, 16), piece)
+        from_line(p + both)
+
+        @pl.when(p >= both)
+        def _():
+            q = jnp.maximum(p - both, 0)
+            landed(from_peer.at[z, q], peer_recv.at[z, q])
+            acc[...] += from_peer[z, q].astype(f32)
+
+        if both:
+            @pl.when(p < both)
+            def _():
+                q = jnp.minimum(p, both - 1)
+                landed(from_closing.at[q], closing_recv.at[q])
+                acc[...] += from_closing[q].astype(f32)
+
+        out_ref[pl.ds(mult(p * piece, piece), piece), :] = (stream[at, :] + acc[...]).astype(bf16)
         return carry
 
     lax.fori_loop(0, pieces, finish, 0)
@@ -1028,32 +1156,26 @@
         def _():
             kv_up(chip).wait_send()
 
-        def sent(k, size, on_line, crosses):
-            def line():
+        def sent(k, start, size, on_line, crosses):
+            if on_line:
                 @pl.when((chip <= z) & (z < last))
                 def _():
-                    row_copy(chip, k, size, row_up, above).wait_send()
+                    row_copy(chip, k, start, size, row_up, above).wait_send()
 
                 @pl.when((chip >= z) & (z > 0))
                 def _():
-                    row_copy(chip, k, size, row_down, below).wait_send()
-
-            if on_line:
-                line()
+                    row_copy(chip, k, start, size, row_down, below).wait_send()
+
             if crosses:
-                @pl.when(chip != z)
-                def _():
-                    row_copy(chip, k, size, row_peer, peer).wait_send()
-
-            row_copy(chip, k, size, row_core, other).wait_send()
+                row_copy(chip, k, start, size, row_peer, peer).wait_send()
+
+            row_copy(chip, k, start, size, row_core, other).wait_send()
 
         for t in range(own):
-            sent(own * x + t, chunk, True, True)
-            sent(own * (1 - x) + t, chunk, False, False)
-        for t in range(shared):
-            sent(2 * own + t, chunk, True, False)
-        if tail:
-            sent(full, tail, True, False)
+            sent(own_id(x, t), own_at(x, t), chunk, True, True)
+            sent(own_id(1 - x, t), own_at(1 - x, t), chunk, False, False)
+        for k, start, size in spread_over:
+            sent(k, start, size, True, False)
 
         @pl.when((chip <= z) & (z < last))
         def _():
@@ -1066,28 +1188,33 @@
         meta_copy(chip, meta_core, other).wait_send()
         for r in range(2 * pieces):
             part_copy(chip, r).wait_send()
-        for r in range(pieces):
+        for r in range(pieces - both):
             cross_copy(chip, r).wait_send()
-
+        for u in range(slots):
             @pl.when(chip > z)
             def _():
-                up_hop(chip, r).wait_send()
+                hop_copy(0, chip, u).wait_send()
 
             @pl.when(chip < z)
             def _():
-                down_hop(chip, r).wait_send()
+                hop_copy(1, chip, u).wait_send()
 
         return carry
 
     lax.fori_loop(0, chips, drain, 0)
-    for k in order:
-        parts_copy(k).wait_send()
+    for t in range(own):
+        parts_copy(t, own_at(1 - x, t), chunk).wait_send()
+    for n, (k, start, size) in enumerate(spread_over):
+        parts_copy(own + n, start, size).wait_send()
+    squares_copy.wait_send()
+    for u in range(both):
+        last_copy(u).wait_send()
 
 
 def whole_layer(
     dims, sinks, ids, route, gain, queries, keys_values, residual, project, gate_up, down
 ):
-    chips, pairs, chunk, piece = dims
+    chips, pairs, chunk, piece, own, both = dims
     cores = 2
     width, depth = residual.shape
     kv_groups = keys_values.shape[1] // (2 * HEAD_DIM)
@@ -1096,7 +1223,7 @@
     hidden = down.shape[0]
     half = width // 2
     pieces = half // piece
-    count = -(-width // chunk)
+    count = -(-width // chunk) + 2
     bf16, f32 = jnp.bfloat16, jnp.float32
     dma = pltpu.SemaphoreType.DMA
     vmem = pltpu.VMEM
@@ -1135,17 +1262,22 @@
             vmem((chips, 2 * pieces, piece, depth), bf16),
             vmem((chips, 2 * pieces, piece, depth), bf16),
             vmem((chips, 2 * pieces, piece, depth), bf16),
-            vmem((chips, pieces, piece, depth), bf16),
-            vmem((chips, pieces, piece, depth), bf16),
-            vmem((chips, pieces, piece, depth), bf16),
-            vmem((chips, pieces, piece, depth), bf16),
-            vmem((chips, pieces, piece, depth), bf16),
+            vmem((chips, max(pieces - both, 1), piece, depth), bf16),
+            vmem((chips, max(pieces - both, 1), piece, depth), bf16),
+            vmem((chips, pieces + both, piece, depth), bf16),
+            vmem((2, chips, pieces + both, piece, depth), bf16),
+            vmem((max(both, 1), piece, depth), bf16),
+            vmem((max(both, 1), piece, depth), bf16),
+            vmem((piece, depth), f32),
+            vmem((8, depth), f32),
+            vmem((8, depth), f32),
             dma((kv_groups + 5,)),
             dma((chips, cores)),
             dma((chips,)),
             dma((chips,)),
             dma((count,)),
             dma((count,)),
+            dma((2,)),
             dma((chips, cores, count)),
             dma((chips, count)),
             dma((chips, count)),
@@ -1157,11 +1289,12 @@
             dma((chips,)),
             dma((chips, 2 * pieces)),
             dma((chips, 2 * pieces)),
-            dma((chips, pieces)),
-            dma((chips, pieces)),
-            dma((chips, pieces)),
-            dma((chips, pieces)),
-            dma((chips, pieces)),
+            dma((chips, max(pieces - both, 1))),
+            dma((chips, max(pieces - both, 1))),
+            dma((chips, pieces + both)),
+            dma((2, chips, pieces + both)),
+            dma((max(both, 1),)),
+            dma((max(both, 1),)),
         ],
         compiler_params=pltpu.CompilerParams(
             collective_id=0, has_side_effects=True, vmem_limit_bytes=VMEM_BYTES
@@ -1192,8 +1325,10 @@
     half = width // 2
     chunk = min(512, half // 128 * 128)
     piece = next(n for n in (480, 240, 160, 80, 48, 32, 16, half) if half % n == 0)
+    own = max(width // chunk // 2 - OWN_LESS, 1)
+    both = min(BOTH, half // piece - 1)
     out = whole_layer(
-        (chips, pairs, chunk, piece),
+        (chips, pairs, chunk, piece, own, both),
         sink_logits,
         expert_ids.T,
         route_weights.T,

time: 136 us -> 110 us (0.81)
  Pallas kernels: 133 us -> 106 us
    pallas_call x1, Pallas kernels: 133 us -> 106 us  [whole_layer(): pl.pallas_call(functools.partial(layer_kernel, dims), out_shape=jax.Shape...]
where the time goes in v2:
time: 110 us; the launch traced here: 109 us
  Pallas kernels  106 us (96%)
  local copies, waits for them, and re-layouts  3.06 us (3%)
    pallas_call x1, Pallas kernels, whole_layer(): pl.pallas_call(functools.partial(layer_kernel, dims), out_shape=jax.Shape...  106 us

profile of v2, /device:TPU:0, one launch (start us, length us, event | category | flops | bytes accessed | tf_op | source)
XLA Modules:
  0.0 109.4 jit_solution(6971779474463811439)
XLA Ops:
  0.0 1.3 %broadcast_in_dim.3.gain_ref = f32[1,2880]{1,0:T(1,128)} reshape(f32[2880]{0:T(1024)} %param.15) | data formatting | bytes 23040 | tf_op jit(solution)/shard_map/broadcast_in_dim | solution.py:1335
  1.3 106.4 %shard_map.100 = bf16[1440,128]{1,0:T(8,128)(2,1)} custom-call(f32[32]{0:T(128)} %sink_ref.1, s32[4,128]{1,0:T(4,128)} %bitcast.14, f32[4,128]{1,0:T(4,128)} %bitcast.15, f32[1,2880]{1,0:T(1,128)} %broadcast_in_dim.3.gain_ref, bf16[128,2048]{1,0:T(8,128)(2,1)} %query_hbm.1, bf16[128,512]{1,0:T(8,128)(2,1)} %kv_hbm.1, bf16[2880,128]{1,0:T(8,128)(2,1)} %bitcast.13, ...), custom_call_target="tpu_custom_call" | custom-call | flops 14250147840 | bytes 24238080 | tf_op jit(solution)/shard_map/pallas_call | solution.py:1234
  107.7 1.7 %copy.12 = bf16[128,1440]{0,1:T(8,128)(2,1)} copy(bf16[128,1440]{0,1:T(8,128)(2,1)} %bitcast.9) | data formatting | bytes 737280

commit v3 on v2

--- a/solution.py
+++ b/solution.py
@@ -13,7 +13,7 @@
 
 VMEM_BYTES = 67_043_328
 OWN_LESS = 0
-BOTH = 1
+BOTH = 0
 
 
 def moe_kernel(
@@ -637,32 +637,32 @@
     sides = jnp.where(z > 0, 1, 0) + jnp.where(z < last, 1, 0)
     pl.semaphore_wait(barrier, sides + 2)
 
-    def kv_up(chip):
-        slot = kvs.at[chip * cores + c]
-        return remote(slot, slot, kv_up_send.at[chip], kv_recv.at[chip, c], above)
-
-    def kv_core(chip):
-        slot = kvs.at[chip * cores + c]
-        return remote(slot, slot, kv_core_send.at[chip], kv_recv.at[chip, c], other)
-
-    def kv_wait(chip, core):
-        landed(kvs.at[chip * cores + core], kv_recv.at[chip, core])
-
-    def kv_pass(chip):
+    def kv_up(chip, g):
+        slot = kvs.at[chip * cores + c, g]
+        return remote(slot, slot, kv_up_send.at[chip, g], kv_recv.at[chip, c, g], above)
+
+    def kv_core(chip, g):
+        slot = kvs.at[chip * cores + c, g]
+        return remote(slot, slot, kv_core_send.at[chip, g], kv_recv.at[chip, c, g], other)
+
+    def kv_wait(chip, core, g):
+        landed(kvs.at[chip * cores + core, g], kv_recv.at[chip, core, g])
+
+    def kv_pass(chip, g):
         @pl.when(z < last)
         def _():
-            kv_up(chip).start()
-
-        kv_core(chip).start()
-
-    for load in loads:
+            kv_up(chip, g).start()
+
+        kv_core(chip, g).start()
+
+    for g, load in enumerate(loads):
         load.wait()
-    kv_pass(z)
+        kv_pass(z, g)
 
     for b in range(-(-width // 128)):
         size = min(128, width - b * 128)
-        gain = gain_ref[:, b * 128:b * 128 + size]
-        gain_cols[b * 128:b * 128 + size, :] = jnp.broadcast_to(gain, (128, size)).T
+        gain = gain_ref[b * 128:b * 128 + size]
+        gain_cols[b * 128:b * 128 + size, :] = jnp.broadcast_to(gain[None, :], (128, size)).T
 
     bulk[0].wait()
     for g in range(kv_groups):
@@ -710,20 +710,18 @@
             accum[g, :, lane] = sums[:, lane] * decay + more
 
     def attend_chip(chip, masked):
-        kv_wait(chip, 1 - c)
-
         def group(g, carry):
+            kv_wait(chip, 1 - c, g)
             attend(chip, g, masked)
+
+            @pl.when(chip > 0)
+            def _():
+                kv_wait(chip - 1, c, g)
+                kv_pass(chip - 1, g)
+
             return carry
 
-        lax.fori_loop(0, kv_groups // 2, group, 0)
-
-        @pl.when(chip > 0)
-        def _():
-            kv_wait(chip - 1, c)
-            kv_pass(chip - 1)
-
-        lax.fori_loop(kv_groups // 2, kv_groups, group, 0)
+        lax.fori_loop(0, kv_groups, group, 0)
 
     attend_chip(z, True)
 
@@ -813,8 +811,12 @@
 
     bulk[1].wait()
     bulk[2].wait()
-    for t in range(own):
+
+    def give_own(t, carry):
         give(t, own_at(1 - x, t), chunk)
+        return carry
+
+    lax.fori_loop(0, own, give_own, 0)
     squares_own = jnp.zeros((8, depth), f32)
     squares_all = jnp.zeros((8, depth), f32)
     for t in range(own):
@@ -883,12 +885,14 @@
 
         each_side(i, act)
 
-    def pump_all(i):
+    def pump_own(i):
         def one(t, carry):
             pump(i, own_id(x, t), own_at(x, t), chunk, True)
             return carry
 
         lax.fori_loop(0, own, one, 0)
+
+    def pump_shared(i):
         for k, start, size in spread_over:
             pump(i, k, start, size, False)
 
@@ -1060,33 +1064,36 @@
         finish_rows(z)
 
     bulk[4].wait()
-    pump_all(0)
+    pump_own(0)
+    pump_shared(0)
 
     def step(i, carry):
         chip = chip_at(i)
         multiply_line(chip)
+        pump_own(i)
         each_side(i - 1, cross_in)
         multiply_crossed(chip)
 
         @pl.when(jnp.logical_not(is_end))
         def _():
-            pump_all(i)
-
-        @pl.when(i > 1)
-        def _():
-            hops(i - 1, True)
+            pump_shared(i)
 
         def between():
             @pl.when(is_end)
             def _():
-                pump_all(i)
-
-            @pl.when(i == jnp.where(is_end, last, 1))
-            def _():
-                for t in range(own):
-                    row_copy(z, own_id(x, t), own_at(x, t), chunk, row_peer, peer).start()
+                pump_shared(i)
 
         finish_rows(chip, between)
+
+        @pl.when(i == jnp.where(is_end, last, 1))
+        def _():
+            for t in range(own):
+                row_copy(z, own_id(x, t), own_at(x, t), chunk, row_peer, peer).start()
+
+        @pl.when(i > 1)
+        def _():
+            hops(i - 1, True)
+
         return carry
 
     lax.fori_loop(1, chips, step, 0)
@@ -1148,13 +1155,14 @@
     lax.fori_loop(0, pieces, finish, 0)
 
     def drain(chip, carry):
-        @pl.when(chip <= z)
-        def _():
-            kv_core(chip).wait_send()
-
-        @pl.when((chip <= z) & (z < last))
-        def _():
-            kv_up(chip).wait_send()
+        for g in range(kv_groups):
+            @pl.when(chip <= z)
+            def _():
+                kv_core(chip, g).wait_send()
+
+            @pl.when((chip <= z) & (z < last))
+            def _():
+                kv_up(chip, g).wait_send()
 
         def sent(k, start, size, on_line, crosses):
             if on_line:
@@ -1272,9 +1280,9 @@
             vmem((8, depth), f32),
             vmem((8, depth), f32),
             dma((kv_groups + 5,)),
-            dma((chips, cores)),
-            dma((chips,)),
-            dma((chips,)),
+            dma((chips, cores, kv_groups)),
+            dma((chips, kv_groups)),
+            dma((chips, kv_groups)),
             dma((count,)),
             dma((count,)),
             dma((2,)),
@@ -1332,7 +1340,7 @@
         sink_logits,
         expert_ids.T,
         route_weights.T,
-        norm_gain[None, :],
+        norm_gain,
         queries,
         keys_values,
         residual.T,

time: 110 us -> 99.8 us (0.907)
  Pallas kernels: 106 us -> 97.8 us
  local copies, waits for them, and re-layouts: 3.06 us -> 1.75 us
    pallas_call x1, Pallas kernels: 106 us -> 97.8 us  [whole_layer(): pl.pallas_call(functools.partial(layer_kernel, dims), out_shape=jax.Shape...]
    broadcast_in_dim x1 -> x0, local copies, waits for them, and re-layouts: 1.31 us -> none  [per_device_whole(): norm_gain[None, :]]
where the time goes in v3:
time: 99.8 us; the launch traced here: 99.5 us
  Pallas kernels  97.8 us (98%)
  local copies, waits for them, and re-layouts  1.75 us (2%)
    pallas_call x1, Pallas kernels, whole_layer(): pl.pallas_call(functools.partial(layer_kernel, dims), out_shape=jax.Shape...  97.8 us

profile of v3, /device:TPU:0, one launch (start us, length us, event | category | flops | bytes accessed | tf_op | source)
XLA Modules:
  0.0 99.5 jit_solution(5231197214863418997)
XLA Ops:
  0.0 97.8 %shard_map.100 = bf16[1440,128]{1,0:T(8,128)(2,1)} custom-call(f32[32]{0:T(128)} %sink_ref.1, s32[4,128]{1,0:T(4,128)} %bitcast.14, f32[4,128]{1,0:T(4,128)} %bitcast.15, f32[2880]{0:T(1024)} %gain_ref.1, bf16[128,2048]{1,0:T(8,128)(2,1)} %query_hbm.1, bf16[128,512]{1,0:T(8,128)(2,1)} %kv_hbm.1, bf16[2880,128]{1,0:T(8,128)(2,1)} %bitcast.13, ...), custom_call_target="tpu_custom_call" | custom-call | flops 14250147840 | bytes 24238080 | tf_op jit(solution)/shard_map/pallas_call | solution.py:1242
  97.8 1.7 %copy.12 = bf16[128,1440]{0,1:T(8,128)(2,1)} copy(bf16[128,1440]{0,1:T(8,128)(2,1)} %bitcast.9) | data formatting | bytes 737280

commit v4 on v3

--- a/solution.py
+++ b/solution.py
@@ -12,8 +12,10 @@
 MESH_ID = pl.DeviceIdType.MESH
 
 VMEM_BYTES = 67_043_328
-OWN_LESS = 0
-BOTH = 0
+CHUNK = 512
+PIECE = 240
+JOINT = 2
+OWN = 2
 
 
 def moe_kernel(
@@ -534,9 +536,9 @@
     cross,
     from_peer,
     hop,
+    relay,
     inbox,
-    closing,
-    from_closing,
+    wide,
     acc,
     squares,
     peer_squares,
@@ -561,11 +563,12 @@
     peer_send,
     peer_recv,
     hop_send,
+    relay_recv,
     inbox_recv,
-    closing_send,
-    closing_recv,
+    wide_send,
+    wide_recv,
 ):
-    chips, pairs, chunk, piece, own, both = dims
+    chips, pairs, chunk, piece, own = dims
     cores = 2
     width, depth = residual_hbm.shape
     kv_groups = kvs.shape[1]
@@ -578,6 +581,7 @@
         edges.append((far + own * chunk, width - far - own * chunk))
     spread_over = [(2 * own + n, at, size) for n, (at, size) in enumerate(edges)]
     pieces = half // piece
+    joint = next(n for n in range(JOINT, 0, -1) if pieces % n == 0)
     last = chips - 1
 
     tok = lax.axis_index("tok")
@@ -915,8 +919,10 @@
         row_wait(chip, 1 - c, k, start, size)
         at = pl.ds(start, size)
         pair = jnp.concatenate([rows[chip, c, at, :], rows[chip, 1 - c, at, :]], axis=1)
+        units = hidden.shape[0] // 2
         for side in range(2):
-            hidden[side] += jnp.dot(gate_w[side, :, at], pair, preferred_element_type=f32)
+            lot = slice(side * units, (side + 1) * units)
+            hidden[lot] += jnp.dot(gate_w[lot, at], pair, preferred_element_type=f32)
 
     def multiply_line(chip):
         hidden[...] = jnp.zeros(hidden.shape, f32)
@@ -948,129 +954,160 @@
             peer_recv.at[chip, r], peer,
         )
 
-    def hop_copy(way, chip, u):
+    def far_end(chip):
+        return chip == jnp.where(chip > z, last, 0)
+
+    def adds(chip):
+        return far_end(chip) & (jnp.where(chip > z, z, last - z) % 2 == 1) & (chip != partner)
+
+    def relay_copy(chip, u):
         return remote(
-            hop.at[chip, u], inbox.at[way, chip, u], hop_send.at[chip, u],
-            inbox_recv.at[way, chip, u], {"tok": tok + cores * (1 - 2 * way)},
-        )
-
-    def last_copy(u):
+            hop.at[chip, u], relay.at[chip, u], hop_send.at[chip, u],
+            relay_recv.at[chip, u], {"tok": tok + jnp.where(chip > z, cores, -cores)},
+        )
+
+    def final_copy(chip, u):
         return remote(
-            closing.at[u], from_closing.at[u], closing_send.at[u], closing_recv.at[u], peer
-        )
-
-    def piece_of(u):
-        return jnp.where(u < both, (1 - x) * pieces + u, x * pieces + u - both)
-
-    slots = pieces + both
-    nearer = jnp.where(z < last - z, 0, 1)
-
-    def hops(i, ends):
-        def toward(turn_of, carry):
-            way = jnp.where(nearer == 0, turn_of, 1 - turn_of)
-            chip = jnp.where(way == 0, i, last - i)
-            incoming = jnp.where(way == 0, z, last - z) > 0
-            sends = jnp.where(way == 0, chip - z, z - chip) > 0
-            if ends is not None:
-                sends = sends & (incoming != ends)
-
-            def one(u, carry):
-                at = piece_of(u)
-                @pl.when(u >= 2 * both)
-                def _():
-                    r = jnp.maximum(u - 2 * both, 0)
-                    landed(from_peer.at[chip, r], peer_recv.at[chip, r])
-                    acc[...] = kept[chip, at].astype(f32) + from_peer[chip, r].astype(f32)
-
-                @pl.when(u < 2 * both)
-                def _():
-                    acc[...] = kept[chip, at].astype(f32)
-
-                @pl.when(incoming)
-                def _():
-                    landed(inbox.at[way, chip, u], inbox_recv.at[way, chip, u])
-                    acc[...] += inbox[way, chip, u].astype(f32)
-
-                hop[chip, u] = acc[...].astype(bf16)
-                hop_copy(way, chip, u).start()
-                return carry
-
-            @pl.when(sends)
+            hop.at[chip, u], inbox.at[z, u], hop_send.at[chip, u],
+            inbox_recv.at[z, u], {"tok": chip * cores + c},
+        )
+
+    partner = z + 1 - 2 * (z % 2)
+
+    def wide_copy(at):
+        return remote(
+            kept.at[partner, at], wide.at[at], wide_send.at[at], wide_recv.at[at],
+            {"tok": partner * cores + c},
+        )
+
+    def send_sum(chip):
+        direct = adds(chip) | jnp.logical_not(far_end(chip))
+
+        def one(u, carry):
+            landed(from_peer.at[chip, u], peer_recv.at[chip, u])
+            acc[...] = kept[chip, x * pieces + u].astype(f32) + from_peer[chip, u].astype(f32)
+
+            @pl.when(adds(chip))
             def _():
-                lax.fori_loop(0, slots, one, 0)
+                landed(relay.at[chip, u], relay_recv.at[chip, u])
+                acc[...] += relay[chip, u].astype(f32)
+
+            hop[chip, u] = acc[...].astype(bf16)
+
+            @pl.when(direct)
+            def _():
+                final_copy(chip, u).start()
+
+            @pl.when(jnp.logical_not(direct))
+            def _():
+                relay_copy(chip, u).start()
 
             return carry
 
-        lax.fori_loop(0, 2, toward, 0)
-
-    def finish_rows(chip, between=None):
+        lax.fori_loop(0, pieces, one, 0)
+
+    def send_own_sum(chip):
+        @pl.when((chip != partner) & jnp.logical_not(adds(chip)))
+        def _():
+            send_sum(chip)
+
+    def activate(chip):
         meta_wait(chip, 1 - c)
         scale = jnp.concatenate([meta[chip, c, 0:1, :], meta[chip, 1 - c, 0:1, :]], axis=1)
         weight = jnp.concatenate(
             [meta[chip, c, pl.ds(8 + tok, 1), :], meta[chip, 1 - c, pl.ds(8 + tok, 1), :]], axis=1
         )
-        gate = hidden[0] * scale
-        up = hidden[1] * scale
+        units = hidden.shape[0] // 2
+        gate = hidden[:units] * scale
+        up = hidden[units:] * scale
         active[...] = (gate * jax.nn.sigmoid(1.702 * gate) * (up + 1.0) * weight).astype(bf16)
 
-        def spread(r, carry):
-            at = jnp.where(r < pieces, (1 - x) * pieces + r, x * pieces + r - pieces)
+    def spread_out(chip, between=None):
+        def spread(n, carry):
+            first = joint * n
+            first = jnp.where(first < pieces, (1 - x) * pieces + first, x * pieces + first - pieces)
             value = jnp.dot(
-                down_t[pl.ds(mult(at * piece, piece), piece), :], active[...],
+                down_t[pl.ds(mult(first * piece, 16), joint * piece), :], active[...],
                 preferred_element_type=f32,
             )
-            part[chip, at] = value[:, depth:].astype(bf16)
-            part_copy(chip, at).start()
-            kept[chip, at] = value[:, :depth].astype(bf16)
+            for m in range(joint):
+                at = first + m
+                block = value[m * piece:(m + 1) * piece]
+                part[chip, at] = block[:, depth:].astype(bf16)
+                part_copy(chip, at).start()
+                kept[chip, at] = block[:, :depth].astype(bf16)
             return carry
 
-        lax.fori_loop(0, 2 * pieces, spread, 0)
+        lax.fori_loop(0, 2 * pieces // joint, spread, 0)
         if between is not None:
             between()
 
-        def join(r, carry):
+        def summed(at):
+            landed(from_core.at[chip, at], part_recv.at[chip, at])
+            acc[...] = kept[chip, at].astype(f32) + from_core[chip, at].astype(f32)
+
+            @pl.when(chip == z)
+            def _():
+                landed(wide.at[at], wide_recv.at[at])
+                acc[...] += wide[at].astype(f32)
+
+        def keep(at):
+            kept[chip, at] = acc[...].astype(bf16)
+
+            @pl.when(chip == partner)
+            def _():
+                wide_copy(at).start()
+
+        def give_half(r, carry):
             at = (1 - x) * pieces + r
-            landed(from_core.at[chip, at], part_recv.at[chip, at])
-            value = kept[chip, at].astype(f32) + from_core[chip, at].astype(f32)
-
-            @pl.when(r >= both)
+            summed(at)
+
+            @pl.when(chip == partner)
             def _():
-                cross[chip, jnp.maximum(r - both, 0)] = value.astype(bf16)
-                cross_copy(chip, jnp.maximum(r - both, 0)).start()
-
-            @pl.when(r < both)
+                keep(at)
+
+            @pl.when(chip != partner)
             def _():
-                kept[chip, at] = value.astype(bf16)
+                cross[chip, r] = acc[...].astype(bf16)
+                cross_copy(chip, r).start()
 
             return carry
 
-        lax.fori_loop(0, pieces, join, 0)
-
-        def keep(r, carry):
-            at = x * pieces + r
-            landed(from_core.at[chip, at], part_recv.at[chip, at])
-            value = kept[chip, at].astype(f32) + from_core[chip, at].astype(f32)
-            kept[chip, at] = value.astype(bf16)
+        lax.fori_loop(0, pieces, give_half, 0)
+
+        def keep_half(r, carry):
+            summed(x * pieces + r)
+            keep(x * pieces + r)
             return carry
 
-        lax.fori_loop(0, pieces, keep, 0)
+        lax.fori_loop(0, pieces, keep_half, 0)
 
     is_end = (z == 0) | (z == last)
-
-    def own_block():
-        multiply_line(z)
-        cross_in(z)
-        multiply_crossed(z)
-        finish_rows(z)
+    early = z < chips // 2
+
+    def own_across():
+        for t in range(own):
+            row_copy(z, own_id(x, t), own_at(x, t), chunk, row_peer, peer).start()
+
+    @pl.when(early)
+    def _():
+        own_across()
 
     bulk[4].wait()
     pump_own(0)
     pump_shared(0)
 
+    @pl.when(jnp.logical_not(early))
+    def _():
+        own_across()
+
+
     def step(i, carry):
         chip = chip_at(i)
         multiply_line(chip)
+
         pump_own(i)
+
         each_side(i - 1, cross_in)
         multiply_crossed(chip)
 
@@ -1083,73 +1120,46 @@
             def _():
                 pump_shared(i)
 
-        finish_rows(chip, between)
-
-        @pl.when(i == jnp.where(is_end, last, 1))
-        def _():
-            for t in range(own):
-                row_copy(z, own_id(x, t), own_at(x, t), chunk, row_peer, peer).start()
+        activate(chip)
+        spread_out(chip, between)
 
         @pl.when(i > 1)
         def _():
-            hops(i - 1, True)
+            send_own_sum(chip_at(i - 1))
 
         return carry
 
     lax.fori_loop(1, chips, step, 0)
-
-    @pl.when(jnp.logical_not(is_end))
-    def _():
-        own_block()
-
-    for i in range(1, last):
-        hops(i, False)
-    hops(last, None)
-
-    @pl.when(is_end)
-    def _():
-        own_block()
-
-    def from_line(u):
-        acc[...] = kept[z, piece_of(u)].astype(f32)
-
-        @pl.when(z > 0)
-        def _():
-            landed(inbox.at[0, z, u], inbox_recv.at[0, z, u])
-            acc[...] += inbox[0, z, u].astype(f32)
-
-        @pl.when(z < last)
-        def _():
-            landed(inbox.at[1, z, u], inbox_recv.at[1, z, u])
-            acc[...] += inbox[1, z, u].astype(f32)
-
-    def closes(u, carry):
-        from_line(u)
-        closing[u] = acc[...].astype(bf16)
-        last_copy(u).start()
+    multiply_line(z)
+    cross_in(z)
+    multiply_crossed(z)
+    activate(z)
+    spread_out(z)
+    send_own_sum(chip_at(last))
+
+    def send_added(i, carry):
+        @pl.when(adds(chip_at(i)))
+        def _():
+            send_sum(chip_at(i))
+
         return carry
 
-    lax.fori_loop(0, both, closes, 0)
+    lax.fori_loop(1, chips, send_added, 0)
 
     def finish(r, carry):
-        p = jnp.where(r < pieces - both, r + both, r - (pieces - both))
-        at = pl.ds(mult(x * half + p * piece, 16), piece)
-        from_line(p + both)
-
-        @pl.when(p >= both)
-        def _():
-            q = jnp.maximum(p - both, 0)
-            landed(from_peer.at[z, q], peer_recv.at[z, q])
-            acc[...] += from_peer[z, q].astype(f32)
-
-        if both:
-            @pl.when(p < both)
+        at = pl.ds(mult(x * half + r * piece, 16), piece)
+        landed(from_peer.at[z, r], peer_recv.at[z, r])
+        acc[...] = kept[z, x * pieces + r].astype(f32) + from_peer[z, r].astype(f32)
+        for src in range(chips):
+            below_it = (src < z) & ((z < last) | (src % 2 == 1))
+            above_it = (src > z) & ((z > 0) | ((last - src) % 2 == 1))
+
+            @pl.when((below_it | above_it) & (src != partner))
             def _():
-                q = jnp.minimum(p, both - 1)
-                landed(from_closing.at[q], closing_recv.at[q])
-                acc[...] += from_closing[q].astype(f32)
-
-        out_ref[pl.ds(mult(p * piece, piece), piece), :] = (stream[at, :] + acc[...]).astype(bf16)
+                landed(inbox.at[src, r], inbox_recv.at[src, r])
+                acc[...] += inbox[src, r].astype(f32)
+
+        out_ref[pl.ds(mult(r * piece, piece), piece), :] = (stream[at, :] + acc[...]).astype(bf16)
         return carry
 
     lax.fori_loop(0, pieces, finish, 0)
@@ -1196,16 +1206,20 @@
         meta_copy(chip, meta_core, other).wait_send()
         for r in range(2 * pieces):
             part_copy(chip, r).wait_send()
-        for r in range(pieces - both):
-            cross_copy(chip, r).wait_send()
-        for u in range(slots):
-            @pl.when(chip > z)
-            def _():
-                hop_copy(0, chip, u).wait_send()
-
-            @pl.when(chip < z)
-            def _():
-                hop_copy(1, chip, u).wait_send()
+        @pl.when(chip != partner)
+        def _():
+            for r in range(pieces):
+                cross_copy(chip, r).wait_send()
+
+        @pl.when(chip == partner)
+        def _():
+            for r in range(2 * pieces):
+                wide_copy(r).wait_send()
+
+        @pl.when((chip != z) & (chip != partner))
+        def _():
+            for u in range(pieces):
+                final_copy(chip, u).wait_send()
 
         return carry
 
@@ -1215,14 +1229,12 @@
     for n, (k, start, size) in enumerate(spread_over):
         parts_copy(own + n, start, size).wait_send()
     squares_copy.wait_send()
-    for u in range(both):
-        last_copy(u).wait_send()
 
 
 def whole_layer(
     dims, sinks, ids, route, gain, queries, keys_values, residual, project, gate_up, down
 ):
-    chips, pairs, chunk, piece, own, both = dims
+    chips, pairs, chunk, piece, own = dims
     cores = 2
     width, depth = residual.shape
     kv_groups = keys_values.shape[1] // (2 * HEAD_DIM)
@@ -1265,17 +1277,17 @@
             vmem((width, depth), bf16),
             vmem((chips, cores, width, depth), bf16),
             vmem((chips, cores, 8 + experts, depth), f32),
-            vmem((2, hidden, cores * depth), f32),
+            vmem((2 * hidden, cores * depth), f32),
             vmem((hidden, cores * depth), bf16),
             vmem((chips, 2 * pieces, piece, depth), bf16),
             vmem((chips, 2 * pieces, piece, depth), bf16),
             vmem((chips, 2 * pieces, piece, depth), bf16),
-            vmem((chips, max(pieces - both, 1), piece, depth), bf16),
-            vmem((chips, max(pieces - both, 1), piece, depth), bf16),
-            vmem((chips, pieces + both, piece, depth), bf16),
-            vmem((2, chips, pieces + both, piece, depth), bf16),
-            vmem((max(both, 1), piece, depth), bf16),
-            vmem((max(both, 1), piece, depth), bf16),
+            vmem((chips, pieces, piece, depth), bf16),
+            vmem((chips, pieces, piece, depth), bf16),
+            vmem((chips, pieces, piece, depth), bf16),
+            vmem((chips, pieces, piece, depth), bf16),
+            vmem((chips, pieces, piece, depth), bf16),
+            vmem((2 * pieces, piece, depth), bf16),
             vmem((piece, depth), f32),
             vmem((8, depth), f32),
             vmem((8, depth), f32),
@@ -1297,12 +1309,13 @@
             dma((chips,)),
             dma((chips, 2 * pieces)),
             dma((chips, 2 * pieces)),
-            dma((chips, max(pieces - both, 1))),
-            dma((chips, max(pieces - both, 1))),
-            dma((chips, pieces + both)),
-            dma((2, chips, pieces + both)),
-            dma((max(both, 1),)),
-            dma((max(both, 1),)),
+            dma((chips, pieces)),
+            dma((chips, pieces)),
+            dma((chips, pieces)),
+            dma((chips, pieces)),
+            dma((chips, pieces)),
+            dma((2 * pieces,)),
+            dma((2 * pieces,)),
         ],
         compiler_params=pltpu.CompilerParams(
             collective_id=0, has_side_effects=True, vmem_limit_bytes=VMEM_BYTES
@@ -1331,12 +1344,11 @@
     pairs = lax.axis_size("pair")
     chips = lax.axis_size("tok") // 2
     half = width // 2
-    chunk = min(512, half // 128 * 128)
-    piece = next(n for n in (480, 240, 160, 80, 48, 32, 16, half) if half % n == 0)
-    own = max(width // chunk // 2 - OWN_LESS, 1)
-    both = min(BOTH, half // piece - 1)
+    chunk = min(CHUNK, half // 128 * 128)
+    piece = next(n for n in (PIECE, 160, 80, 48, 32, 16, half) if half % n == 0)
+    own = min(OWN, half // chunk)
     out = whole_layer(
-        (chips, pairs, chunk, piece, own, both),
+        (chips, pairs, chunk, piece, own),
         sink_logits,
         expert_ids.T,
         route_weights.T,
@@ -1345,7 +1357,7 @@
         keys_values,
         residual.T,
         out_weight.T,
-        jnp.transpose(gate_up[0], (1, 2, 0)),
+        jnp.transpose(gate_up[0], (1, 2, 0)).reshape(2 * down_weight.shape[1], width),
         down_weight[0],
     )
     return out.T
@@ -1365,7 +1377,7 @@
         P("tok", ("head", "pair"), None),
     )
     sizes = mesh.shape
-    chip_pair = sizes["pair"] == 1 and sizes["head"] == 2 and sizes["tok"] % 2 == 0
+    chip_pair = sizes["pair"] == 1 and sizes["head"] == 2 and sizes["tok"] % 4 == 0
     return jax.shard_map(
         per_device_whole if chip_pair else per_device,
         mesh=mesh,

time: 99.8 us -> 93.9 us (0.941)
  Pallas kernels: 97.8 us -> 91.9 us
    pallas_call x1, Pallas kernels: 97.8 us -> 91.9 us  [whole_layer(): pl.pallas_call(functools.partial(layer_kernel, dims), out_shape=jax.Shape...]
where the time goes in v4:
time: 93.9 us; the launch traced here: 93.7 us
  Pallas kernels  91.9 us (98%)
  local copies, waits for them, and re-layouts  1.75 us (2%)
    pallas_call x1, Pallas kernels, whole_layer(): pl.pallas_call(functools.partial(layer_kernel, dims), out_shape=jax.Shape...  91.9 us

profile of v4, /device:TPU:0, one launch (start us, length us, event | category | flops | bytes accessed | tf_op | source)
XLA Modules:
  0.0 93.7 jit_solution(743583846504481598)
XLA Ops:
  0.0 91.9 %shard_map.100 = bf16[1440,128]{1,0:T(8,128)(2,1)} custom-call(f32[32]{0:T(128)} %sink_ref.1, s32[4,128]{1,0:T(4,128)} %bitcast.16, f32[4,128]{1,0:T(4,128)} %bitcast.17, f32[2880]{0:T(1024)} %gain_ref.1, bf16[128,2048]{1,0:T(8,128)(2,1)} %query_hbm.1, bf16[128,512]{1,0:T(8,128)(2,1)} %kv_hbm.1, bf16[2880,128]{1,0:T(8,128)(2,1)} %bitcast.15, ...), custom_call_target="tpu_custom_call" | custom-call | flops 14250147840 | bytes 24238080 | tf_op jit(solution)/shard_map/pallas_call | solution.py:1254
  92.0 1.7 %copy.12 = bf16[128,1440]{0,1:T(8,128)(2,1)} copy(bf16[128,1440]{0,1:T(8,128)(2,1)} %bitcast.11) | data formatting | bytes 737280

commit v5 on v4

--- a/solution.py
+++ b/solution.py
@@ -13,8 +13,8 @@
 
 VMEM_BYTES = 67_043_328
 CHUNK = 512
-PIECE = 240
-JOINT = 2
+PIECE = 480
+JOINT = 1
 OWN = 2
 
 
@@ -980,7 +980,7 @@
             {"tok": partner * cores + c},
         )
 
-    def send_sum(chip):
+    def send_sum(chip, low, high):
         direct = adds(chip) | jnp.logical_not(far_end(chip))
 
         def one(u, carry):
@@ -1004,12 +1004,12 @@
 
             return carry
 
-        lax.fori_loop(0, pieces, one, 0)
-
-    def send_own_sum(chip):
+        lax.fori_loop(low, high, one, 0)
+
+    def send_own_sum(chip, low, high):
         @pl.when((chip != partner) & jnp.logical_not(adds(chip)))
         def _():
-            send_sum(chip)
+            send_sum(chip, low, high)
 
     def activate(chip):
         meta_wait(chip, 1 - c)
@@ -1108,12 +1108,16 @@
 
         pump_own(i)
 
+        @pl.when(jnp.logical_not(is_end))
+        def _():
+            pump_shared(i)
+
         each_side(i - 1, cross_in)
         multiply_crossed(chip)
 
-        @pl.when(jnp.logical_not(is_end))
-        def _():
-            pump_shared(i)
+        @pl.when(i > 1)
+        def _():
+            send_own_sum(chip_at(i - 1), 0, pieces // 2)
 
         def between():
             @pl.when(is_end)
@@ -1125,7 +1129,7 @@
 
         @pl.when(i > 1)
         def _():
-            send_own_sum(chip_at(i - 1))
+            send_own_sum(chip_at(i - 1), pieces // 2, pieces)
 
         return carry
 
@@ -1134,13 +1138,19 @@
     cross_in(z)
     multiply_crossed(z)
     activate(z)
-    spread_out(z)
-    send_own_sum(chip_at(last))
+    cuts = [pieces * n // 3 for n in range(4)]
+
+    def send_last(n):
+        send_own_sum(chip_at(last), cuts[n], cuts[n + 1])
+
+    send_last(0)
+    spread_out(z, lambda: send_last(1))
+    send_last(2)
 
     def send_added(i, carry):
         @pl.when(adds(chip_at(i)))
         def _():
-            send_sum(chip_at(i))
+            send_sum(chip_at(i), 0, pieces)
 
         return carry
 

time: 93.9 us -> 91.2 us (0.971)
  Pallas kernels: 91.9 us -> 89.2 us
    pallas_call x1, Pallas kernels: 91.9 us -> 89.2 us  [whole_layer(): pl.pallas_call(functools.partial(layer_kernel, dims), out_shape=jax.Shape...]
where the time goes in v5:
time: 91.2 us; the launch traced here: 91 us
  Pallas kernels  89.2 us (98%)
  local copies, waits for them, and re-layouts  1.75 us (2%)
    pallas_call x1, Pallas kernels, whole_layer(): pl.pallas_call(functools.partial(layer_kernel, dims), out_shape=jax.Shape...  89.2 us

profile of v5, /device:TPU:0, one launch (start us, length us, event | category | flops | bytes accessed | tf_op | source)
XLA Modules:
  0.0 91.0 jit_solution(5235275294157654592)
XLA Ops:
  0.0 89.2 %shard_map.100 = bf16[1440,128]{1,0:T(8,128)(2,1)} custom-call(f32[32]{0:T(128)} %sink_ref.1, s32[4,128]{1,0:T(4,128)} %bitcast.16, f32[4,128]{1,0:T(4,128)} %bitcast.17, f32[2880]{0:T(1024)} %gain_ref.1, bf16[128,2048]{1,0:T(8,128)(2,1)} %query_hbm.1, bf16[128,512]{1,0:T(8,128)(2,1)} %kv_hbm.1, bf16[2880,128]{1,0:T(8,128)(2,1)} %bitcast.15, ...), custom_call_target="tpu_custom_call" | custom-call | flops 14250147840 | bytes 24238080 | tf_op jit(solution)/shard_map/pallas_call | solution.py:1264
  89.2 1.7 %copy.12 = bf16[128,1440]{0,1:T(8,128)(2,1)} copy(bf16[128,1440]{0,1:T(8,128)(2,1)} %bitcast.11) | data formatting | bytes 737280

commit v6 on v5

--- a/solution.py
+++ b/solution.py
@@ -663,11 +663,6 @@
         load.wait()
         kv_pass(z, g)
 
-    for b in range(-(-width // 128)):
-        size = min(128, width - b * 128)
-        gain = gain_ref[b * 128:b * 128 + size]
-        gain_cols[b * 128:b * 128 + size, :] = jnp.broadcast_to(gain[None, :], (128, size)).T
-
     bulk[0].wait()
     for g in range(kv_groups):
         query_t[g, HEAD_DIM:, :] = jnp.zeros((HEAD_DIM, repeat * depth), bf16)
@@ -828,6 +823,11 @@
         for n, (k, start, size) in enumerate(spread_over):
             if t == 0:
                 hold(start, size, give(own + n, start, size))
+        if t == 0:
+            for b in range(-(-width // 128)):
+                size = min(128, width - b * 128)
+                gain = gain_ref[b * 128:b * 128 + size]
+                gain_cols[b * 128:b * 128 + size, :] = jnp.broadcast_to(gain[None, :], (128, size)).T
         squares_own += settle(t, own_id(x, t), own_at(x, t), chunk)
     squares[...] = squares_own
     squares_copy = remote(squares, peer_squares, squares_sem.at[0], squares_sem.at[1], peer)
@@ -1134,18 +1134,18 @@
         return carry
 
     lax.fori_loop(1, chips, step, 0)
+    cuts = [pieces * n // 3 for n in range(4)]
+
+    def send_last(n):
+        send_own_sum(chip_at(last), cuts[n], cuts[n + 1])
+
     multiply_line(z)
+    send_last(0)
     cross_in(z)
     multiply_crossed(z)
     activate(z)
-    cuts = [pieces * n // 3 for n in range(4)]
-
-    def send_last(n):
-        send_own_sum(chip_at(last), cuts[n], cuts[n + 1])
-
-    send_last(0)
-    spread_out(z, lambda: send_last(1))
-    send_last(2)
+    send_last(1)
+    spread_out(z, lambda: send_last(2))
 
     def send_added(i, carry):
         @pl.when(adds(chip_at(i)))

time: 91.2 us -> 91.4 us (level)
  no operation moved by 1% of the time
where the time goes in v6:
time: 91.4 us; the launch traced here: 91.2 us
  Pallas kernels  89.5 us (98%)
  local copies, waits for them, and re-layouts  1.75 us (2%)
    pallas_call x1, Pallas kernels, whole_layer(): pl.pallas_call(functools.partial(layer_kernel, dims), out_shape=jax.Shape...  89.5 us

profile of v6, /device:TPU:0, one launch (start us, length us, event | category | flops | bytes accessed | tf_op | source)
XLA Modules:
  0.0 91.2 jit_solution(11973900301717363108)
XLA Ops:
  0.0 89.5 %shard_map.100 = bf16[1440,128]{1,0:T(8,128)(2,1)} custom-call(f32[32]{0:T(128)} %sink_ref.1, s32[4,128]{1,0:T(4,128)} %bitcast.16, f32[4,128]{1,0:T(4,128)} %bitcast.17, f32[2880]{0:T(1024)} %gain_ref.1, bf16[128,2048]{1,0:T(8,128)(2,1)} %query_hbm.1, bf16[128,512]{1,0:T(8,128)(2,1)} %kv_hbm.1, bf16[2880,128]{1,0:T(8,128)(2,1)} %bitcast.15, ...), custom_call_target="tpu_custom_call" | custom-call | flops 14250147840 | bytes 24238080 | tf_op jit(solution)/shard_map/pallas_call | solution.py:1264
  89.5 1.7 %copy.12 = bf16[128,1440]{0,1:T(8,128)(2,1)} copy(bf16[128,1440]{0,1:T(8,128)(2,1)} %bitcast.11) | data formatting | bytes 737280
